TPU v7x, 32 devices: a whole 2x2x4 slice. The times are simulated.
32 devices in a mesh: dp: 16 (over z, x, core), tile: 2 (over y).
Axes of the slice: x: 2, y: 2, z: 4, core: 2. Of those that a mesh axis runs over, the one named last changes fastest.
Arguments:
- proposal_boxes: int32 [16, 4, 512], P('dp'), may hold values from 0 to 672, as said below
- level_plan: int32 [16, 512], P('dp'), may hold values from 0 to 1
- fine_map: bfloat16 [16, 84, 168, 128], P('dp', 'tile'), may hold values from -6 to 6
- coarse_map: bfloat16 [16, 42, 84, 128], P('dp', 'tile'), may hold values from -6 to 6
- first_weight: bfloat16 [6272, 1024], P('tile', 'dp'), may hold values from -0.078125 to 0.078125
- second_weight: bfloat16 [1024, 1024], P('tile', 'dp'), may hold values from -0.1875 to 0.1875
- upstream: bfloat16 [16, 512, 1024], P('dp'), may hold values from -6 to 6
Outputs:
- first_grad: float32 [6272, 1024], P('tile', 'dp')
- second_grad: float32 [1024, 1024], P('tile', 'dp')
Inputs may be any that keep to these rules, and one draw needn't show every extreme that they name: `proposal_boxes`: with s = 4 where level_plan is 0 and s = 8 where it is 1: h >= 1, w >= 1, y0 + h <= 336, x0 + w <= 672, (y0 mod s) + h <= 14 * s and (x0 mod s) + w <= 14 * s. Band b holds the proposals with b * 168 <= y0 < (b + 1) * 168; at most 256 of an image's proposals lie in one band, and in every image some band holds exactly 256.
All inputs are finite; a program needn't handle non-finite values.
Results may differ from a plain program's by a relative error of at most 0.017.
Values may be sent and summed in bfloat16 or wider, within the bound.
A program may use at most 64 MiB of HBM per device.

v0:
```python
import functools

import jax
import jax.numpy as jnp
from jax import lax
from jax.experimental import pallas as pl
from jax.experimental.pallas import tpu as pltpu
from jax.sharding import PartitionSpec as P

WIN = 16
BINS = 7
ROWS_PAD = 56
GROUP = 16


def from_ahead(block, axis, distance):
    if distance == 0:
        return block
    size = lax.axis_size(axis)
    return lax.ppermute(block, axis, [(i, (i - distance) % size) for i in range(size)])


def halo_from_next(block, axis):
    size = lax.axis_size(axis)
    return lax.ppermute(block, axis, [(i + 1, i) for i in range(size - 1)])


def gelu_parts(hidden):
    factor = 0.7978845608028654
    cubic_term = 0.044715
    inner_term = factor * (hidden + cubic_term * hidden * hidden * hidden)
    tangent = jnp.tanh(inner_term)
    gelu_value = 0.5 * hidden * (1.0 + tangent)
    gelu_slope = 0.5 * (1.0 + tangent) + 0.5 * hidden * (1.0 - tangent * tangent) * factor * (
        1.0 + 3.0 * cubic_term * hidden * hidden
    )
    return (gelu_value, gelu_slope)


def crop_kernel(starts, width, cells_ref, geo_ref, maps_ref, out_ref, wide, stage):
    step = pl.program_id(0)

    @pl.when(step == 0)
    def _():
        def widen(r, carry):
            wide[r] = maps_ref[r].astype(jnp.float32)
            return carry

        lax.fori_loop(0, maps_ref.shape[0], widen, 0)

    shape = (ROWS_PAD, WIN * WIN)
    k = lax.broadcasted_iota(jnp.int32, shape, 0).astype(jnp.float32)
    i_bin = jnp.floor((k + 0.5) * (1.0 / BINS))
    j_bin = k - BINS * i_bin
    i_mid = i_bin + 0.5
    j_mid = j_bin + 0.5
    lane = lax.broadcasted_iota(jnp.int32, shape, 1)
    r_cell = (lane >> 4).astype(jnp.float32)
    q_cell = (lane & 15).astype(jnp.float32)
    for p in range(GROUP):
        n = step * GROUP + p
        row = cells_ref[0, n]
        col = cells_ref[1, n]
        row_w = jnp.maximum(0.0, 1.0 - jnp.abs(i_mid * geo_ref[1, n] + geo_ref[0, n] - r_cell))
        col_w = jnp.maximum(0.0, 1.0 - jnp.abs(j_mid * geo_ref[3, n] + geo_ref[2, n] - q_cell))
        weights = (row_w * col_w).astype(jnp.bfloat16)
        window = jnp.concatenate(
            [wide[row + r, pl.ds(col, WIN), :] for r in range(WIN)], axis=0
        ).astype(jnp.bfloat16)
        crop = jnp.dot(weights, window, preferred_element_type=jnp.float32)
        stage[pl.ds(p, ROWS_PAD, stride=GROUP), :] = crop
    for t, first in enumerate(starts):
        for m in range(width):
            at = (first + m) * GROUP
            out_ref[t, :, m * 128 : (m + 1) * 128] = stage[at : at + GROUP, :].astype(jnp.bfloat16)


def make_crops(cells, geo, maps, starts, width, capacity):
    tiles = len(starts)
    lanes = width * 128
    return pl.pallas_call(
        functools.partial(crop_kernel, starts, width),
        grid=(capacity // GROUP,),
        out_shape=jax.ShapeDtypeStruct((tiles, capacity, lanes), jnp.bfloat16),
        in_specs=[
            pl.BlockSpec(memory_space=pltpu.SMEM),
            pl.BlockSpec(memory_space=pltpu.SMEM),
            pl.BlockSpec(maps.shape, lambda g: (0, 0, 0)),
        ],
        out_specs=pl.BlockSpec((tiles, GROUP, lanes), lambda g: (0, g, 0)),
        scratch_shapes=[
            pltpu.VMEM(maps.shape, jnp.float32),
            pltpu.VMEM((ROWS_PAD * GROUP, 128), jnp.float32),
        ],
        compiler_params=pltpu.CompilerParams(
            dimension_semantics=("arbitrary",), vmem_limit_bytes=48 * 1024 * 1024
        ),
        cost_estimate=pl.CostEstimate(
            flops=capacity * ROWS_PAD * WIN * WIN * 128 * 16,
            bytes_accessed=2 * maps.size + 2 * tiles * capacity * lanes,
            transcendentals=0,
        ),
        name="crops",
    )(cells, geo, maps)


def per_device(
    proposal_boxes, level_plan, fine_map, coarse_map, first_weight, second_weight, upstream
):
    tile_count = lax.axis_size("tile")
    band = lax.axis_index("tile")
    num_props = level_plan.shape[1]
    capacity = max(num_props // 4, num_props // tile_count)
    fine_tile = fine_map[0]
    coarse = coarse_map[0]
    fine_rows, fine_cols, channels = fine_tile.shape
    coarse_rows, coarse_cols = (coarse.shape[0], coarse.shape[1])

    top_rows = jnp.concatenate([fine_tile[:WIN], coarse[:WIN]], axis=1)
    below_rows = halo_from_next(top_rows, "tile")

    share_feats = first_weight.shape[0]
    feats = share_feats * tile_count
    width = max(
        -(-((t + 1) * share_feats) // 128) - t * share_feats // 128 for t in range(tile_count)
    )
    starts = [min(t * share_feats // 128, feats // 128 - width) for t in range(tile_count)]
    lanes = width * 128
    feat_off = band * share_feats - 128 * jnp.minimum(
        band * share_feats // 128, feats // 128 - width
    )

    first_rows = lax.dynamic_update_slice(
        jnp.zeros((first_weight.shape[1], lanes), jnp.bfloat16),
        first_weight.T,
        (0, feat_off),
    )
    both = lax.all_gather(
        jnp.concatenate([first_rows, second_weight.T], axis=1), "dp", axis=0, tiled=True
    )
    first_all = both[:, :lanes]
    second_all = both[:, lanes:]

    fields = proposal_boxes[0]
    levels = level_plan[0]
    owner = fields[0] // (4 * fine_rows)
    members = (owner[:, None] == jnp.arange(tile_count, dtype=jnp.int32)[None, :]).astype(jnp.int32)
    rank = jnp.sum((jnp.cumsum(members, axis=0) - 1) * members, axis=1)
    relative = lax.rem(owner - band + tile_count, tile_count)
    slot_id = relative * capacity + rank
    slots = tile_count * capacity
    chosen = slot_id[None, :] == jnp.arange(slots, dtype=jnp.int32)[:, None]
    upstream_slots = jnp.dot(
        chosen.astype(jnp.bfloat16), upstream[0], preferred_element_type=jnp.float32
    ).astype(jnp.bfloat16)
    mine = chosen[:capacity].astype(jnp.int32)
    top, left, height, box_width = (
        jnp.sum(mine * fields[f][None, :], axis=1) for f in range(4)
    )
    level = jnp.sum(mine * levels[None, :], axis=1)

    stride = jnp.where(level == 0, 4, 8).astype(jnp.int32)
    is_fine = level == 0
    first_row = top // stride
    local_row = jnp.clip(
        first_row - band * jnp.where(is_fine, fine_rows, coarse_rows),
        0,
        jnp.where(is_fine, fine_rows, coarse_rows) - 1,
    )
    first_col = jnp.minimum(left // stride, jnp.where(is_fine, fine_cols, coarse_cols) - WIN)
    cells = jnp.stack(
        [local_row + jnp.where(is_fine, 0, fine_rows + WIN), first_col], axis=0
    ).astype(jnp.int32)
    stride_float = stride.astype(jnp.float32)
    geo = jnp.stack(
        [
            top.astype(jnp.float32) / stride_float - first_row.astype(jnp.float32),
            height.astype(jnp.float32) / (7.0 * stride_float),
            left.astype(jnp.float32) / stride_float - first_col.astype(jnp.float32),
            box_width.astype(jnp.float32) / (7.0 * stride_float),
        ],
        axis=0,
    )

    side = ((0, 0), (0, fine_cols - coarse_cols), (0, 0))
    maps = jnp.concatenate(
        [
            fine_tile,
            below_rows[:, :fine_cols],
            jnp.pad(coarse, side),
            jnp.pad(below_rows[:, fine_cols:], side),
        ],
        axis=0,
    )
    crop_blocks = make_crops(cells, geo, maps, starts, width, capacity)
    own_feats = jnp.concatenate(
        [
            from_ahead(
                lax.dynamic_index_in_dim(
                    crop_blocks, lax.rem(band - d + tile_count, tile_count), 0, keepdims=False
                ),
                "tile",
                d,
            )
            for d in range(tile_count)
        ],
        axis=0,
    )

    partial_hidden = lax.dot_general(
        own_feats, first_all, (((1,), (1,)), ((), ())), preferred_element_type=jnp.float32
    ).astype(jnp.bfloat16)
    share = second_weight.shape[0]

    def in_my_order(block, d):
        return jnp.roll(block, d * capacity, axis=0) if d else block

    hidden_own = 0.0
    for d in range(tile_count):
        to = lax.rem(band - d + tile_count, tile_count)
        piece = lax.dynamic_slice_in_dim(partial_hidden, to * share, share, axis=1)
        hidden_own = hidden_own + in_my_order(from_ahead(piece, "tile", d), d).astype(jnp.float32)
    gelu_value, gelu_slope = gelu_parts(hidden_own)
    activated = gelu_value.astype(jnp.bfloat16)
    back_grad = jnp.dot(upstream_slots, second_all, preferred_element_type=jnp.float32)
    pre_own = (back_grad * gelu_slope).astype(jnp.bfloat16)
    ahead = [in_my_order(from_ahead(pre_own, "tile", d), d) for d in range(tile_count)]
    twice = jnp.concatenate(ahead + ahead[:-1], axis=1)
    pre_grad = lax.dynamic_slice_in_dim(
        twice, lax.rem(tile_count - band, tile_count) * share, tile_count * share, axis=1
    )
    over_rows = (((0,), (0,)), ((), ()))
    second_part = lax.dot_general(
        upstream_slots, activated, over_rows, preferred_element_type=jnp.float32
    ).astype(jnp.bfloat16)
    first_part = lax.dot_general(
        pre_grad, own_feats, over_rows, preferred_element_type=jnp.float32
    ).astype(jnp.bfloat16)
    summed = lax.psum_scatter(
        jnp.concatenate([first_part, second_part], axis=1), "dp", scatter_dimension=0, tiled=True
    ).astype(jnp.float32)
    first_grad = lax.dynamic_slice_in_dim(summed[:, :lanes], feat_off, share_feats, axis=1).T
    second_grad = summed[:, lanes:].T
    return (first_grad, second_grad)


def solution(mesh):
    placed = (
        P("dp", None, None),
        P("dp", None),
        P("dp", "tile", None, None),
        P("dp", "tile", None, None),
        P("tile", "dp"),
        P("tile", "dp"),
        P("dp", None, None),
    )
    return jax.shard_map(
        per_device,
        mesh=mesh,
        in_specs=placed,
        out_specs=(P("tile", "dp"), P("tile", "dp")),
        check_vma=False,
    )
```

profile of v0, /device:TPU:0, one launch (start us, length us, event | category | flops | bytes accessed | tf_op | source)
XLA Modules:
  0.0 263.4 jit_solution(14502915766918753195)
XLA Ops:
  7.2 0.0 copy-start
  7.2 0.0 slice-start
  7.2 0.0 slice-start.1
  7.2 0.0 all-gather.2.cloned.1.call-start
  7.3 0.0 copy-start.4
  7.3 5.0 %dynamic_update_slice.3 = bf16[64,3200]{1,0:T(8,128)(2,1)S(1)} dynamic-update-slice(bf16[64,3200]{1,0:T(8,128)(2,1)S(1)} %broadcast_in_dim.33, bf16[64,3136]{1,0:T(8,128)(2,1)} %bitcast.56, s32[]{:T(128)} %constant.88.clone.1, s32[]{:T(128)S(6)} %select_n.146) | dynamic-update-slice | bytes 802820 | tf_op jit(solution)/shard_map/dynamic_update_slice | solution.py:133
  12.3 0.0 copy-start.5
  12.3 1.7 pad_maximum_fusion.8
  14.0 0.0 all-gather.2.cloned.1.call-update
  14.0 0.0 reduce-scatter.2.cloned.1.call-start
  14.1 0.1 copy.35
  14.3 1.1 pad_maximum_fusion.6
  15.4 1.3 collective-permute-start
  16.7 0.6 reduce-window.6
  17.4 0.2 slice_reduce_fusion
  17.6 0.2 reduce-window.9
  17.8 0.1 add_bitcast_fusion
  17.9 0.2 iota_compare_fusion.3
  18.1 0.4 select_reduce_fusion.1
  18.6 0.1 select_divide_fusion.1
  18.7 0.1 compare_and_fusion.1
  18.9 24.5 %collective-permute-done = bf16[16,252,128]{2,0,1:T(8,128)(2,1)} collective-permute-done((bf16[16,252,128]{2,0,1:T(8,128)(2,1)}, bf16[16,252,128]{2,0,1:T(8,128)(2,1)}, u32[]{:S(2)}, u32[]{:S(2)}) %collective-permute-start) | collective-permute-done | bytes 1032224 | tf_op jit(solution)/shard_map/ppermute | solution.py:25
  43.4 1.2 slice.94
  44.6 0.2 copy.29
  44.8 1.0 slice.95
  45.8 0.1 copy.30
  45.9 8.8 %fusion.6.maps_ref = bf16[95,168,128]{2,1,0:T(8,128)(2,1)} fusion(bf16[16,84,128]{2,1,0:T(8,128)(2,1)S(1)} %copy.30, bf16[21,84,128]{2,1,0:T(8,128)(2,1)} %bitcast.54, bf16[16,168,128]{2,1,0:T(8,128)(2,1)S(1)} %copy.29, bf16[42,168,128]{2,1,0:T(8,128)(2,1)S(1)} %bitcast.52), kind=kLoop, calls=%fused_computation.11 | loop fusion | flops 28600320 | bytes 7375872 | tf_op jit(solution)/shard_map/concatenate | solution.py:186
  54.7 13.2 %crops.1 = bf16[2,256,3200]{2,1,0:T(8,128)(2,1)S(1)} custom-call(s32[2,256]{1,0:T(2,128)S(1)} %pad_add_fusion.cells_ref, f32[4,256]{1,0:T(4,128)S(1)} %pad_maximum_fusion.10.geo_ref, bf16[95,168,128]{2,1,0:T(8,128)(2,1)} %fusion.6.maps_ref), custom_call_target="tpu_custom_call" | custom-call | flops 7516192768 | bytes 7362560 | tf_op jit(solution)/shard_map/crops/pallas_call | solution.py:81
  67.9 1.4 dynamic-slice_bitcast_fusion.1
  69.3 37.3 %collective-permute-done.1 = bf16[256,3200]{1,0:T(8,128)(2,1)} collective-permute-done((bf16[256,3200]{1,0:T(8,128)(2,1)}, bf16[256,3200]{1,0:T(8,128)(2,1)}, u32[]{:S(2)}, u32[]{:S(2)}) %collective-permute-start.1) | collective-permute-done | bytes 1638432 | tf_op jit(solution)/shard_map/ppermute | solution.py:20
  106.6 7.1 %fusion.7 = bf16[512,1024]{0,1:T(8,128)(2,1)S(1)} fusion(bf16[1024,3712]{1,0:T(8,128)(2,1)} %all-gather.2.cloned.1.call-done, bf16[256,3200]{1,0:T(8,128)(2,1)} %collective-permute-done.1, bf16[256,3200]{1,0:T(8,128)(2,1)S(1)} %get-tuple-element.11), kind=kOutput, calls=%fused_computation.23 | convolution fusion | flops 3362521088 | bytes 10878976 | tf_op jit(solution)/shard_map/dot_general | solution.py:210
  113.7 1.0 copy-done.2
  114.6 0.8 constant_dynamic-slice_fusion
  115.5 0.3 collective-permute-start.2
  115.8 0.7 convolution_convert_fusion.1
  116.5 11.4 %collective-permute-done.2 = bf16[512,512]{0,1:T(8,128)(2,1)S(1)} collective-permute-done((bf16[512,512]{0,1:T(8,128)(2,1)}, bf16[512,512]{0,1:T(8,128)(2,1)S(1)}, u32[]{:S(2)}, u32[]{:S(2)}) %collective-permute-start.2) | collective-permute-done | bytes 524320 | tf_op jit(solution)/shard_map/ppermute | solution.py:20
  128.0 3.6 %fusion.10 = bf16[512,512]{0,1:T(8,128)(2,1)} fusion(bf16[512,1024]{1,0:T(8,128)(2,1)S(1)} %convolution_convert_fusion.1, bf16[1024,3712]{1,0:T(8,128)(2,1)} %all-gather.2.cloned.1.call-done, bf16[512,1024]{0,1:T(8,128)(2,1)} %copy-done.2, s32[]{:T(128)S(6)} %select_n.156, bf16[256,512]{0,1:T(8,128)(2,1)S(1)} %get-tuple-element.16, ...), kind=kOutput, calls=%fused_computation.25 | convolution fusion | flops 543424512 | bytes 3670020 | tf_op jit(solution)/shard_map/dot_general | solution.py:225
  131.6 0.6 collective-permute-start.3
  132.1 3.3 %convolution_convert_fusion.2 = bf16[1024,512]{1,0:T(8,128)(2,1)} fusion(bf16[512,1024]{1,0:T(8,128)(2,1)} %copy-done.6, bf16[512,1024]{0,1:T(8,128)(2,1)} %copy-done.2, s32[]{:T(128)S(6)} %select_n.156, bf16[256,512]{0,1:T(8,128)(2,1)} %copy-done.3, bf16[256,512]{0,1:T(8,128)(2,1)S(1)} %get-tuple-element.15), kind=kOutput, calls=%fused_computation.22 | convolution fusion | flops 541327360 | bytes 3145732 | tf_op jit(solution)/shard_map/dot_general | solution.py:233
  135.5 7.7 %collective-permute-done.3 = bf16[512,512]{0,1:T(8,128)(2,1)S(1)} collective-permute-done((bf16[512,512]{0,1:T(8,128)(2,1)}, bf16[512,512]{0,1:T(8,128)(2,1)S(1)}, u32[]{:S(2)}, u32[]{:S(2)}) %collective-permute-start.3) | collective-permute-done | bytes 524320 | tf_op jit(solution)/shard_map/ppermute | solution.py:20
  143.2 9.2 %convolution_convert_fusion = bf16[1024,3200]{1,0:T(8,128)(2,1)} fusion(bf16[256,3200]{1,0:T(8,128)(2,1)} %collective-permute-done.1, bf16[256,3200]{1,0:T(8,128)(2,1)S(1)} %get-tuple-element.11, s32[]{:T(128)S(6)} %select_n.158, bf16[512,512]{0,1:T(8,128)(2,1)} %fusion.10, bf16[256,512]{0,1:T(8,128)(2,1)S(1)} %get-tuple-element.14, ...), kind=kOutput, calls=%fused_computation.7 | convolution fusion | flops 3369467904 | bytes 10878980 | tf_op jit(solution)/shard_map/dot_general | solution.py:236
  152.5 6.7 %pad_maximum_fusion = bf16[1024,3712]{1,0:T(8,128)(2,1)} fusion(bf16[1024,512]{1,0:T(8,128)(2,1)} %convolution_convert_fusion.2, bf16[1024,3200]{1,0:T(8,128)(2,1)} %convolution_convert_fusion), kind=kLoop, calls=%fused_computation.6 | loop fusion | flops 15204352 | bytes 15204352 | tf_op jit(solution)/shard_map/concatenate | solution.py:240
  159.2 0.0 reduce-scatter.2.cloned.1.call-update
  159.2 93.3 %reduce-scatter.2.cloned.1.call-done = bf16[64,3712]{1,0:T(8,128)(2,1)} async-done(((bf16[1024,3712]{1,0:T(8,128)(2,1)}), bf16[64,3712]{1,0:T(8,128)(2,1)}) %reduce-scatter.2.cloned.1.call-update) | async-done | bytes 475152 | tf_op jit(solution)/shard_map/reduce_scatter | solution.py:239
  252.5 1.1 slice.101
  253.6 1.2 dynamic-slice_bitcast_fusion.2
  254.8 1.1 convert_element_type.147
  255.9 0.7 slice_bitcast_fusion
  (32 shorter events, 0.4 us)
Async XLA Ops:
  7.2 108.6 %copy-start = (bf16[1,512,1024]{2,1,0:T(8,128)(2,1)S(1)}, bf16[1,512,1024]{2,1,0:T(8,128)(2,1)}, u32[]{:S(2)}) copy-start(bf16[1,512,1024]{2,1,0:T(8,128)(2,1)} %param.13) | copy-start | bytes 3145732
  7.2 6.9 %slice-start = ((bf16[1,42,168,128]{3,2,1,0:T(8,128)(2,1)}), bf16[1,16,168,128]{3,2,1,0:T(8,128)(2,1)S(1)}, s32[]{:S(2)}) async-start(bf16[1,42,168,128]{3,2,1,0:T(8,128)(2,1)} %param.9), calls=%async_computation.3 | async-start | bytes 1376256 | tf_op jit(solution)/shard_map/slice | solution.py:119
  7.2 7.0 %slice-start.1 = ((bf16[1,21,84,128]{3,2,1,0:T(8,128)(2,1)}), bf16[1,16,84,128]{3,2,1,0:T(8,128)(2,1)S(1)}, s32[]{:S(2)}) async-start(bf16[1,21,84,128]{3,2,1,0:T(8,128)(2,1)} %param.10), calls=%async_computation.4 | async-start | bytes 720896 | tf_op jit(solution)/shard_map/slice | solution.py:119
  7.2 99.4 %all-gather.2.cloned.1.call-start = ((), (), s32[]{:S(2)}) async-start(), calls=%async_computation.1 | async-start | bytes 8077312 | tf_op jit(solution)/shard_map/all_gather | solution.py:138
  7.3 9.3 %copy-start.4 = (s32[1,4,512]{2,1,0:T(4,128)S(1)}, s32[1,4,512]{2,1,0:T(4,128)}, u32[]{:S(2)}) copy-start(s32[1,4,512]{2,1,0:T(4,128)} %param.7) | copy-start | bytes 24580
  12.3 5.8 %copy-start.5 = (s32[1,512]{1,0:T(1,128)S(1)}, s32[1,512]{1,0:T(1,128)}, u32[]{:S(2)}) copy-start(s32[1,512]{1,0:T(1,128)} %param.8) | copy-start | bytes 6148
  14.0 238.5 %reduce-scatter.2.cloned.1.call-start = ((), (), s32[]{:S(2)}) async-start(), calls=%async_computation.2 | async-start | bytes 8077312 | tf_op jit(solution)/shard_map/reduce_scatter | solution.py:239
  14.2 31.7 %copy-start.1 = (bf16[1,42,168,128]{3,2,1,0:T(8,128)(2,1)S(1)}, bf16[1,42,168,128]{3,2,1,0:T(8,128)(2,1)}, u32[]{:S(2)}) copy-start(bf16[1,42,168,128]{3,2,1,0:T(8,128)(2,1)} %param.9) | copy-start | bytes 5419012
  15.4 28.0 %collective-permute-start = (bf16[16,252,128]{2,0,1:T(8,128)(2,1)}, bf16[16,252,128]{2,0,1:T(8,128)(2,1)}, u32[]{:S(2)}, u32[]{:S(2)}) collective-permute-start(bf16[16,252,128]{2,0,1:T(8,128)(2,1)} %pad_maximum_fusion.6), channel_id=1, source_target_pairs={{1,0},{3,2},{5,4},{7,6},{9,8},{11,10},{13,12},{15,14},{17,16},{19,... | collective-permute-start | bytes 3096584 | tf_op jit(solution)/shard_map/ppermute | solution.py:25
  69.3 37.3 %collective-permute-start.1 = (bf16[256,3200]{1,0:T(8,128)(2,1)}, bf16[256,3200]{1,0:T(8,128)(2,1)}, u32[]{:S(2)}, u32[]{:S(2)}) collective-permute-start(bf16[256,3200]{1,0:T(8,128)(2,1)} %get-tuple-element.12), channel_id=1, source_target_pairs={{0,1},{1,0},{2,3},{3,2},{4,5},{5,4},{6,7},{7,6},{8,9},{9,8},{10,11... | collective-permute-start | bytes 4915208 | tf_op jit(solution)/shard_map/ppermute | solution.py:20
  113.7 1.0 copy-start.2
  115.5 12.5 %collective-permute-start.2 = (bf16[512,512]{0,1:T(8,128)(2,1)}, bf16[512,512]{0,1:T(8,128)(2,1)S(1)}, u32[]{:S(2)}, u32[]{:S(2)}) collective-permute-start(bf16[512,512]{0,1:T(8,128)(2,1)} %constant_dynamic-slice_fusion), channel_id=1, source_target_pairs={{0,1},{1,0},{2,3},{3,2},{4,5},{5,4},{6,7},{7,6},{8,9},{9,8},{10,11... | collective-permute-start | bytes 1572872 | tf_op jit(solution)/shard_map/ppermute | solution.py:20
  116.5 15.1 %copy-start.6 = (bf16[512,1024]{1,0:T(8,128)(2,1)}, bf16[512,1024]{1,0:T(8,128)(2,1)S(1)}, u32[]{:S(2)}) copy-start(bf16[512,1024]{1,0:T(8,128)(2,1)S(1)} %convolution_convert_fusion.1) | copy-start | bytes 3145732
  128.0 3.6 %copy-start.3 = (bf16[256,512]{0,1:T(8,128)(2,1)}, bf16[256,512]{0,1:T(8,128)(2,1)S(1)}, u32[]{:S(2)}) copy-start(bf16[256,512]{0,1:T(8,128)(2,1)S(1)} %get-tuple-element.16) | copy-start | bytes 786436
  131.6 11.6 %collective-permute-start.3 = (bf16[512,512]{0,1:T(8,128)(2,1)}, bf16[512,512]{0,1:T(8,128)(2,1)S(1)}, u32[]{:S(2)}, u32[]{:S(2)}) collective-permute-start(bf16[512,512]{0,1:T(8,128)(2,1)} %fusion.10), channel_id=1, source_target_pairs={{0,1},{1,0},{2,3},{3,2},{4,5},{5,4},{6,7},{7,6},{8,9},{9,8},{10,11... | collective-permute-start | bytes 1572872 | tf_op jit(solution)/shard_map/ppermute | solution.py:20
Sparse Core Ops, SparseCore 0:
  14.1 72.6 all-gather.1
  159.3 93.1 reduce-scatter.1
where the time goes:
time: 264 us; the launch traced here: 263 us
  waiting for transfers between devices  174 us (66%)
  matrix products  24 us (9%)
  other arithmetic  21.3 us (8%)
  between operations  14.4 us (5%)
  local copies, waits for them, and re-layouts  14.1 us (5%)
  Pallas kernels  13.2 us (5%)
    reduce_scatter x1, waiting for transfers between devices, per_device(): lax.psum_scatter(jnp.concatenate([first_part, second_part], axis=1), 'dp'...  93.3 us
    ppermute x3, waiting for transfers between devices, from_ahead(): lax.ppermute(block, axis, [(i, (i - distance) % size) for i in range(size)])  56.4 us
    ppermute x1, waiting for transfers between devices, halo_from_next(): return lax.ppermute(block, axis, [(i + 1, i) for i in range(size - 1)])  24.5 us
    pallas_call x1, Pallas kernels, make_crops(): pl.pallas_call(functools.partial(crop_kernel, starts, width), grid=(capac...  13.2 us
    dot_general x1, matrix products, per_device(): lax.dot_general(pre_grad, own_feats, over_rows, preferred_element_type=jn...  9.24 us
    concatenate x1, other arithmetic, per_device(): jnp.concatenate([fine_tile, below_rows[:, :fine_cols], jnp.pad(coarse, si...  8.77 us
    dot_general x1, matrix products, per_device(): lax.dot_general(own_feats, first_all, (((1,), (1,)), ((), ())), preferred...  7.07 us
    concatenate x1, other arithmetic, per_device(): jnp.concatenate([first_part, second_part], axis=1)  6.72 us
  transfers between devices with their start and end apart: 6, of which 5 were waited for; matrix products, arithmetic and copies ran while one was open for 8% of the time, Pallas kernels for 5%

commit v1 on v0

--- a/solution.py
+++ b/solution.py
@@ -104,7 +104,7 @@
     )(cells, geo, maps)
 
 
-def per_device(
+def per_device_by_bands(
     proposal_boxes, level_plan, fine_map, coarse_map, first_weight, second_weight, upstream
 ):
     tile_count = lax.axis_size("tile")
@@ -244,6 +244,828 @@
     return (first_grad, second_grad)
 
 
+MESH = pl.DeviceIdType.MESH
+REACH = 15
+HALO = REACH - 1
+NT = (((1,), (1,)), ((), ()))
+NN = (((1,), (0,)), ((), ()))
+
+
+def chip_grid(mesh):
+    chips = [getattr(device, "coords", None) for device in mesh.devices[:, 0]]
+    if chips[0] is None:
+        return None
+    cores = sum(1 for c in chips if tuple(c) == tuple(chips[0]))
+    chips = [tuple(c) for c in chips[::cores]]
+    if len(chips) == 1:
+        return (1, 1, cores)
+    axis = [a != b for a, b in zip(chips[0], chips[1])].index(True)
+    fast = 1
+    while fast < len(chips) and all(
+        a == b or i == axis for i, (a, b) in enumerate(zip(chips[0], chips[fast]))
+    ):
+        fast += 1
+    return (len(chips) // fast, fast, cores)
+
+
+def offsets(size):
+    if size == 1:
+        return [0]
+    if size == 2:
+        return [0, 1]
+    return [0] + [s * d for d in range(1, size) for s in (-1, 1)]
+
+
+def steps_of(size):
+    return {1: [], 2: [1]}.get(size, [-1, 1])
+
+
+def moved(position, size, rel):
+    if rel == 0 or size == 1:
+        return position
+    return 1 - position if size == 2 else position + rel
+
+
+def last_axis(order, rel):
+    used = [j for j in range(3) if rel[order[j]]]
+    return used[-1] if used else -1
+
+
+def onward(sizes, order, rel):
+    last = last_axis(order, rel)
+    hops = []
+    if last >= 0:
+        axis = order[last]
+        if sizes[axis] > 2 and abs(rel[axis]) < sizes[axis] - 1:
+            hops.append((last, axis, -1 if rel[axis] > 0 else 1))
+    for j in range(last + 1, 3):
+        hops.extend((j, order[j], step) for step in steps_of(sizes[order[j]]))
+    return hops
+
+
+def arrival_order(sizes, routes, extra):
+    import heapq
+    import itertools
+
+    places = list(itertools.product(*(range(n) for n in sizes)))
+    queue, waiting, busy = [], {}, set()
+    seen, tick = {}, itertools.count()
+
+    def start(link, now):
+        if link not in busy and waiting.get(link):
+            busy.add(link)
+            load, arrival = waiting[link].pop(0)
+            heapq.heappush(queue, (now + load, next(tick), link, arrival))
+
+    def arrive(place, route, rel, now):
+        seen.setdefault((route, rel), []).append(now)
+        for _, axis, step in onward(sizes, routes[route][0], rel):
+            target = list(place)
+            target[axis] = moved(place[axis], sizes[axis], step)
+            if not 0 <= target[axis] < sizes[axis]:
+                continue
+            there = list(rel)
+            there[axis] = rel[axis] - step if sizes[axis] > 2 else 1
+            link = (place, axis, step)
+            waiting.setdefault(link, []).append(
+                (routes[route][1], (tuple(target), route, tuple(there)))
+            )
+            start(link, now)
+
+    first = {}
+    for place in places:
+        for route in extra[1]:
+            arrive(place, route, (0, 0, 0), 0.0)
+        if extra[0] and place[2] == 1:
+            waiting.setdefault((place, 2, 1), []).append((extra[0], None))
+            start((place, 2, 1), 0.0)
+        for route in range(len(routes)):
+            if route not in extra[1]:
+                arrive(place, route, (0, 0, 0), 0.0)
+    end = 0.0
+    while queue:
+        now, _, link, arrival = heapq.heappop(queue)
+        end = now
+        busy.discard(link)
+        if arrival is not None:
+            arrive(*arrival, now)
+        start(link, now)
+    key = {event: sum(t) / len(t) for event, t in seen.items()}
+    for _ in range(sum(sizes)):
+        for (route, rel) in list(key):
+            for _, axis, step in onward(sizes, routes[route][0], rel):
+                there = list(rel)
+                there[axis] = rel[axis] - step if sizes[axis] > 2 else 1
+                event = (route, tuple(there))
+                if event in key:
+                    key[event] = max(key[event], key[(route, rel)] + 1e-3)
+    return sorted(key, key=lambda e: (key[e], e)), key, end
+
+
+def slots_of(sizes, order):
+    counts, before = [], 1
+    for j in range(3):
+        n = sizes[order[j]]
+        counts.append(before * (2 * n if n > 2 else 1))
+        before *= n
+    return counts
+
+
+def when(conds, body):
+    if not conds:
+        body()
+        return
+    total = conds[0]
+    for cond in conds[1:]:
+        total = jnp.logical_and(total, cond)
+    pl.when(total)(body)
+
+
+class Routes:
+    def __init__(self, sizes, position, core, cores, orders):
+        self.sizes, self.position = sizes, position
+        self.core, self.cores = core, cores
+        self.orders = orders
+        self.slot_counts = [slots_of(sizes, order) for order in orders]
+
+    def inside(self, axis, rel):
+        if rel == 0 or self.sizes[axis] <= 2:
+            return []
+        p = self.position[axis]
+        return [p < self.sizes[axis] - rel] if rel > 0 else [p >= -rel]
+
+    def valid(self, rel):
+        return sum((self.inside(axis, rel[axis]) for axis in range(3)), [])
+
+    def at(self, rel):
+        return [moved(self.position[a], self.sizes[a], rel[a]) for a in range(3)]
+
+    def device(self, axis, step):
+        there = list(self.position)
+        there[axis] = moved(there[axis], self.sizes[axis], step)
+        return ((there[0] * self.sizes[1] + there[1]) * self.cores + self.core, there[2])
+
+    def back_step(self, order, rel):
+        axis = order[last_axis(order, rel)]
+        return axis, (1 if self.sizes[axis] == 2 or rel[axis] > 0 else -1)
+
+    def number(self, place):
+        return (place[0] * self.sizes[1] + place[1]) * self.sizes[2] + place[2]
+
+    def direction(self, axis, step):
+        return 2 * axis + (1 if step > 0 else 0)
+
+    def gather(self, route, rel, ref_of, send_sems, recv_sems, drain=False):
+        order = self.orders[route]
+
+        def body():
+            place = self.at(rel)
+            ref = ref_of(place)
+            q = self.number(place)
+
+            def hop(axis, step):
+                return pltpu.make_async_remote_copy(
+                    src_ref=ref,
+                    dst_ref=ref,
+                    send_sem=send_sems.at[route, q, self.direction(axis, step)],
+                    recv_sem=recv_sems.at[route, q],
+                    device_id=self.device(axis, step),
+                    device_id_type=MESH,
+                )
+
+            if last_axis(order, rel) >= 0 and not drain:
+                hop(*self.back_step(order, rel)).wait_recv()
+            for _, axis, step in onward(self.sizes, order, rel):
+                copy = hop(axis, step)
+                when(self.inside(axis, step), copy.wait_send if drain else copy.start)
+
+        when(self.valid(rel), body)
+
+    def slot(self, route, phase, side, place):
+        order, counts = self.orders[route], self.slot_counts[route]
+        index = 0
+        for j in range(phase):
+            index = index * self.sizes[order[j]] + place[order[j]]
+        n = self.sizes[order[phase]]
+        if n > 2:
+            index = (index * n + place[order[phase]]) * 2 + (1 if side > 0 else 0)
+        return sum(counts[:phase]) + index
+
+    def scatter(self, route, rel, ref_of, slots, add, send_sems, recv_sems, drain=False):
+        order = self.orders[route]
+
+        def body():
+            place = self.at(rel)
+            ref = ref_of(place)
+            q = self.number(place)
+            if not drain:
+                for phase, axis, step in onward(self.sizes, order, rel):
+                    slot = self.slot(route, phase, step, place)
+
+                    def take(axis=axis, step=step, slot=slot):
+                        pltpu.make_async_remote_copy(
+                            src_ref=ref,
+                            dst_ref=slots.at[slot],
+                            send_sem=send_sems.at[route, q],
+                            recv_sem=recv_sems.at[route, slot],
+                            device_id=self.device(axis, step),
+                            device_id_type=MESH,
+                        ).wait_recv()
+                        add(ref, slots.at[slot])
+
+                    when(self.inside(axis, step), take)
+            phase = last_axis(order, rel)
+            if phase >= 0:
+                axis, step = self.back_step(order, rel)
+                slot = self.slot(route, phase, 1 if self.sizes[axis] == 2 else -step, place)
+                copy = pltpu.make_async_remote_copy(
+                    src_ref=ref,
+                    dst_ref=slots.at[slot],
+                    send_sem=send_sems.at[route, q],
+                    recv_sem=recv_sems.at[route, slot],
+                    device_id=self.device(axis, step),
+                    device_id_type=MESH,
+                )
+                if drain:
+                    copy.wait_send()
+                else:
+                    copy.start()
+
+        when(self.valid(rel), body)
+
+
+def cut(bins, shares):
+    edges = [0]
+    for i in range(1, len(shares) + 1):
+        edges.append(round(bins * sum(shares[:i]) / sum(shares)))
+    return [(a, b - a) for a, b in zip(edges, edges[1:])]
+
+
+ORDERS = ((2, 0, 1), (0, 1, 2), (1, 2, 0), (2, 0, 1))
+GATHER_SHARES = (10, 11, 4)
+SCATTER_SHARES = (6, 16, 3)
+
+
+def step_kernel(
+    grid,
+    cells_ref,
+    geo_ref,
+    w1_ref,
+    w2_ref,
+    up_ref,
+    upt_ref,
+    fine_ref,
+    coarse_ref,
+    first_ref,
+    second_ref,
+    w_in,
+    wbuf,
+    w2buf,
+    fine_low,
+    coarse_low,
+    wide,
+    stage,
+    crops,
+    upb,
+    uptb,
+    back,
+    hidden,
+    acts,
+    pres,
+    grads,
+    seconds,
+    slots_a,
+    slots_b,
+    slots_c,
+    slots_d,
+    out_first,
+    out_second,
+    swap,
+    local_sems,
+    send_sems,
+    recv_sems,
+    sum_send_sems,
+    sum_recv_sems,
+    core_send,
+    core_recv,
+    crop_send,
+    crop_recv,
+):
+    nz, nx, ny, cores = grid
+    sizes = (nz, nx, ny)
+    chips = nz * nx
+    dp = lax.axis_index("dp")
+    y = lax.axis_index("tile")
+    core = dp % cores
+    chip = dp // cores
+    x = chip % nx
+    z = chip // nx
+    position = (z, x, y)
+    other = 1 - core
+    partner = (chip * cores + other, y)
+    routes = Routes(sizes, position, core, cores, ORDERS)
+    share, h = w1_ref.shape
+    lanes = wbuf.shape[2]
+    bins = lanes // 128
+    fine_rows, fine_cols, _ = fine_ref.shape
+    coarse_rows, coarse_cols, _ = coarse_ref.shape
+    capacity = up_ref.shape[0]
+    depth = w2_ref.shape[2]
+    pair = 2 * h
+    feat_bins = crops.shape[1] // 128
+    starts = [min(t * share // 128, feat_bins - bins) for t in range(ny)]
+    start_bin = starts[0] + y * (starts[1] - starts[0])
+    shift = y * share - 128 * start_bin
+    first_parts = cut(bins, GATHER_SHARES)
+    sum_parts = cut(bins, SCATTER_SHARES)
+
+    barrier = pltpu.get_barrier_semaphore()
+    pl.semaphore_signal(barrier, inc=1, device_id=partner, device_id_type=MESH)
+    peers = 1
+    for axis in range(3):
+        for step in steps_of(sizes[axis]):
+            def greet(axis=axis, step=step):
+                pl.semaphore_signal(
+                    barrier, inc=1, device_id=routes.device(axis, step), device_id_type=MESH
+                )
+            near = routes.inside(axis, step)
+            when(near, greet)
+            peers = peers + (near[0].astype(jnp.int32) if near else 1)
+    pl.semaphore_wait(barrier, peers)
+
+    def rows(start, size):
+        return pl.ds(pl.multiple_of(start, size), size)
+
+    w_copy = pltpu.make_async_copy(
+        w1_ref, w_in.at[pl.ds(pl.multiple_of(shift, 16), share), :], local_sems.at[0]
+    )
+    w_copy.start()
+    w2_rows = rows(chip * pair + core * h, h)
+    w2_copy = pltpu.make_async_copy(w2_ref.at[core], w2buf.at[y, w2_rows, :], local_sems.at[1])
+    w2_copy.start()
+    w2_swap = pltpu.make_async_remote_copy(
+        src_ref=w2_ref.at[other],
+        dst_ref=w2buf.at[y, w2_rows, :],
+        send_sem=core_send.at[0],
+        recv_sem=core_recv.at[0],
+        device_id=partner,
+        device_id_type=MESH,
+    )
+    w2_swap.start()
+    fine_copy = pltpu.make_async_copy(
+        fine_ref, fine_low.at[pl.ds(0, fine_rows)], local_sems.at[2]
+    )
+    coarse_copy = pltpu.make_async_copy(
+        coarse_ref, coarse_low.at[pl.ds(0, coarse_rows)], local_sems.at[3]
+    )
+    fine_copy.start()
+    coarse_copy.start()
+
+    gather_routes = [
+        (ORDERS[i], first_parts[i][1] if i < 3 else depth * pair // (h * 128)) for i in range(4)
+    ]
+    halo_load = HALO * (fine_cols + coarse_cols) // h
+    events, times, _ = arrival_order(sizes, gather_routes, (halo_load, (0, 2)))
+
+    def gather_ref(route):
+        if route == 3:
+            return lambda q: w2buf.at[q[2], rows((q[0] * nx + q[1]) * pair, pair), :]
+        first, count = first_parts[route]
+        return lambda q: wbuf.at[
+            q[2], rows((q[0] * nx + q[1]) * h, h), pl.ds(first * 128, count * 128)
+        ]
+
+    def gather(event, drain=False):
+        route, rel = event
+        routes.gather(route, rel, gather_ref(route), send_sems, recv_sems, drain)
+
+    own_rows = rows(chip * h, h)
+    w_copy.wait()
+    pad = lanes - share
+    w_in[pl.ds(pl.multiple_of((1 - y) * share, 16), pad), :] = jnp.zeros((pad, h), jnp.bfloat16)
+    for i in range(bins):
+        block = w_in[128 * i : 128 * (i + 1), :].astype(jnp.float32)
+        wbuf[y, own_rows, 128 * i : 128 * (i + 1)] = block.T.astype(jnp.bfloat16)
+
+    gather((0, (0, 0, 0)))
+    gather((2, (0, 0, 0)))
+    below = routes.device(2, 1)
+    fine_halo = pltpu.make_async_remote_copy(
+        src_ref=fine_ref.at[pl.ds(0, HALO)],
+        dst_ref=fine_low.at[pl.ds(fine_rows, HALO)],
+        send_sem=core_send.at[1],
+        recv_sem=core_recv.at[1],
+        device_id=below,
+        device_id_type=MESH,
+    )
+    coarse_halo = pltpu.make_async_remote_copy(
+        src_ref=coarse_ref.at[pl.ds(0, HALO)],
+        dst_ref=coarse_low.at[pl.ds(coarse_rows, HALO)],
+        send_sem=core_send.at[2],
+        recv_sem=core_recv.at[2],
+        device_id=below,
+        device_id_type=MESH,
+    )
+
+    @pl.when(y == 1)
+    def _():
+        fine_halo.start()
+        coarse_halo.start()
+
+    gather((1, (0, 0, 0)))
+    w2_copy.wait()
+    w2_swap.wait()
+    gather((3, (0, 0, 0)))
+    todo = [e for e in events if e[1] != (0, 0, 0)]
+
+    half = rows(core * capacity, capacity)
+    ups = []
+    for i, (src, dst) in enumerate(((up_ref, upb.at[half, :]), (upt_ref, uptb.at[core]))):
+        ups.append(pltpu.make_async_copy(src, dst, local_sems.at[4 + i]))
+        ups.append(
+            pltpu.make_async_remote_copy(
+                src_ref=src,
+                dst_ref=dst,
+                send_sem=core_send.at[3 + i],
+                recv_sem=core_recv.at[3 + i],
+                device_id=partner,
+                device_id_type=MESH,
+            )
+        )
+    for copy in ups:
+        copy.start()
+
+    coarse_base = fine_rows + HALO
+
+    def widen(low, first, count, base, cols):
+        def one(r, carry):
+            wide[base + r, 0:cols, :] = low[r].astype(jnp.float32)
+            return carry
+
+        lax.fori_loop(first, first + count, one, 0)
+
+    fine_copy.wait()
+    coarse_copy.wait()
+    widen(fine_low, 0, fine_rows, 0, fine_cols)
+    widen(coarse_low, 0, coarse_rows, coarse_base, coarse_cols)
+
+    scale = max(times.values())
+    early = [e for e in todo if times[e] < HALO_TIME * scale]
+    for event in early:
+        gather(event)
+    todo = todo[len(early) :]
+
+    @pl.when(y == 0)
+    def _():
+        fine_halo.wait_recv()
+        coarse_halo.wait_recv()
+        widen(fine_low, fine_rows, HALO, 0, fine_cols)
+        widen(coarse_low, coarse_rows, HALO, coarse_base, coarse_cols)
+
+    @pl.when(y == 1)
+    def _():
+        def clear(r, carry):
+            wide[r] = jnp.zeros(wide.shape[1:], jnp.float32)
+            return carry
+
+        lax.fori_loop(fine_rows, fine_rows + HALO, clear, 0)
+        lax.fori_loop(coarse_base + coarse_rows, coarse_base + coarse_rows + HALO, clear, 0)
+
+    groups = capacity // GROUP
+    during = [e for e in todo if times[e] < CROP_TIME * scale]
+    todo = todo[len(during) :]
+    shape = (ROWS_PAD, REACH * WIN)
+    k = lax.broadcasted_iota(jnp.int32, shape, 0).astype(jnp.float32)
+    i_bin = jnp.floor((k + 0.5) * (1.0 / BINS))
+    j_bin = k - BINS * i_bin
+    i_mid = i_bin + 0.5
+    j_mid = j_bin + 0.5
+    lane = lax.broadcasted_iota(jnp.int32, shape, 1)
+    r_cell = (lane >> 4).astype(jnp.float32)
+    q_cell = (lane & 15).astype(jnp.float32)
+
+    def crop_copy(g):
+        group_rows = rows(core * capacity + g * GROUP, GROUP)
+        return pltpu.make_async_remote_copy(
+            src_ref=crops.at[group_rows, :],
+            dst_ref=crops.at[group_rows, :],
+            send_sem=crop_send.at[g],
+            recv_sem=crop_recv.at[g],
+            device_id=partner,
+            device_id_type=MESH,
+        )
+
+    def crop_group(g, carry):
+        for n, event in enumerate(during):
+            pl.when(g == n * groups // len(during))(functools.partial(gather, event))
+        for p in range(GROUP):
+            n = g * GROUP + p
+            row = cells_ref[0, n]
+            col = cells_ref[1, n]
+            row_w = jnp.maximum(0.0, 1.0 - jnp.abs(i_mid * geo_ref[1, n] + geo_ref[0, n] - r_cell))
+            col_w = jnp.maximum(0.0, 1.0 - jnp.abs(j_mid * geo_ref[3, n] + geo_ref[2, n] - q_cell))
+            weights = (row_w * col_w).astype(jnp.bfloat16)
+            window = jnp.concatenate(
+                [wide[row + r, pl.ds(col, WIN), :] for r in range(REACH)], axis=0
+            ).astype(jnp.bfloat16)
+            crop = jnp.dot(weights, window, preferred_element_type=jnp.float32)
+            stage[pl.ds(p, ROWS_PAD, stride=GROUP), :] = crop
+        group_rows = rows(core * capacity + g * GROUP, GROUP)
+        for m in range(feat_bins):
+            crops[group_rows, m * 128 : (m + 1) * 128] = stage[
+                m * GROUP : (m + 1) * GROUP, :
+            ].astype(jnp.bfloat16)
+
+        @pl.when(g > 0)
+        def _():
+            crop_copy(g - 1).start()
+
+        return carry
+
+    lax.fori_loop(0, groups, crop_group, 0)
+    crop_copy(groups - 1).start()
+
+    for copy in ups:
+        copy.wait()
+    for event in todo:
+        gather(event)
+    for g in range(groups):
+        crop_copy(g).wait()
+
+    for t in range(ny):
+        part = jnp.dot(upb[...], w2buf[t], preferred_element_type=jnp.float32)
+        back[t * depth : (t + 1) * depth, :] = part.T
+
+    hidden[...] = jnp.zeros_like(hidden)
+    chunk = 640 if lanes % 640 == 0 else 128
+    for t in range(ny):
+        def hide(i, carry, t=t):
+            at = pl.multiple_of(i * chunk, 128)
+            from_at = pl.multiple_of(starts[t] * 128 + i * chunk, 128)
+            hidden[...] += lax.dot_general(
+                wbuf[t, :, pl.ds(at, chunk)],
+                crops[:, pl.ds(from_at, chunk)],
+                NT,
+                preferred_element_type=jnp.float32,
+            )
+            return carry
+
+        lax.fori_loop(0, lanes // chunk, hide, 0)
+
+    def gelu(i, carry):
+        at = rows(i * 32, 32)
+        value, slope = gelu_parts(hidden[at, :])
+        acts[at, :] = value.astype(jnp.bfloat16)
+        pres[at, :] = (back[at, :] * slope).astype(jnp.bfloat16)
+        return carry
+
+    lax.fori_loop(0, hidden.shape[0] // 32, gelu, 0)
+    for event in events:
+        gather(event, drain=True)
+
+    sum_routes = [
+        (ORDERS[i], sum_parts[i][1] if i < 3 else depth * pair // (h * 128)) for i in range(4)
+    ]
+    sum_events, _, _ = arrival_order(sizes, sum_routes, (0, ()))
+    sum_events = sum_events[::-1]
+    slot_refs = (slots_a, slots_b, slots_c, slots_d)
+
+    def sum_ref(route):
+        if route == 3:
+            return lambda q: seconds.at[q[2], rows((q[0] * nx + q[1]) * pair, pair), :]
+        first, count = sum_parts[route]
+        return lambda q: grads.at[
+            q[2], rows((q[0] * nx + q[1]) * h, h), pl.ds(first * 128, count * 128)
+        ]
+
+    def add(ref, more):
+        def one(i, carry):
+            at = rows(i * 16, 16)
+            total = ref[at, :].astype(jnp.float32) + more[at, :].astype(jnp.float32)
+            ref[at, :] = total.astype(jnp.bfloat16)
+            return carry
+
+        lax.fori_loop(0, ref.shape[0] // 16, one, 0)
+
+    def scatter(event, drain=False):
+        route, rel = event
+        routes.scatter(
+            route, rel, sum_ref(route), slot_refs[route], add, sum_send_sems, sum_recv_sems, drain
+        )
+
+    def make_grads(t, part):
+        first, count = sum_parts[part]
+        step = max(c for c in range(1, 6) if count % c == 0)
+
+        def one(i, carry):
+            at = pl.multiple_of((first + i * step) * 128, 128)
+            base = starts[0] + t * (starts[1] - starts[0])
+            from_at = pl.multiple_of(base * 128 + at, 128)
+            grads[t, :, pl.ds(at, step * 128)] = jnp.dot(
+                pres[...], crops[:, pl.ds(from_at, step * 128)], preferred_element_type=jnp.float32
+            ).astype(jnp.bfloat16)
+            return carry
+
+        lax.fori_loop(0, count // step, one, 0)
+
+    def leaf(route):
+        order = ORDERS[route]
+        return [
+            e
+            for e in sum_events
+            if e[0] == route and not onward(sizes, order, e[1])
+        ]
+
+    done = []
+
+    def run(chosen):
+        for event in chosen:
+            scatter(event)
+            done.append(event)
+
+    make_grads(1 - y, 1)
+    run(leaf(1))
+    make_grads(1 - y, 0)
+    make_grads(y, 0)
+    run(leaf(0))
+    for part in range(2):
+        for t in range(ny):
+            total = lax.dot_general(
+                uptb[part],
+                acts[t * depth : (t + 1) * depth, part * capacity : (part + 1) * capacity],
+                NT,
+                preferred_element_type=jnp.float32,
+            )
+            if part:
+                total = total + stash[t]
+            if part == 0:
+                stash = (stash if t else []) + [total]
+            else:
+                seconds[t] = total.astype(jnp.bfloat16)
+    run(leaf(3))
+    make_grads(1 - y, 2)
+    make_grads(y, 2)
+    run(leaf(2))
+    make_grads(y, 1)
+    run([e for e in sum_events if e not in done])
+
+    swap[0] = seconds[y, rows(chip * pair + other * h, h), :]
+    second_swap = pltpu.make_async_remote_copy(
+        src_ref=swap.at[0],
+        dst_ref=swap.at[1],
+        send_sem=core_send.at[5],
+        recv_sem=core_recv.at[5],
+        device_id=partner,
+        device_id_type=MESH,
+    )
+    second_swap.start()
+    for i in range(bins):
+        block = grads[y, own_rows, 128 * i : 128 * (i + 1)].astype(jnp.float32)
+        out_first[128 * i : 128 * (i + 1), :] = block.T
+    first_out = pltpu.make_async_copy(
+        out_first.at[pl.ds(pl.multiple_of(shift, 16), share), :], first_ref, local_sems.at[6]
+    )
+    first_out.start()
+    out_second[core] = seconds[y, rows(chip * pair + core * h, h), :].astype(jnp.float32)
+    second_swap.wait()
+    out_second[other] = swap[1].astype(jnp.float32)
+    second_out = pltpu.make_async_copy(out_second, second_ref, local_sems.at[7])
+    second_out.start()
+    for event in sum_events:
+        scatter(event, drain=True)
+
+    @pl.when(y == 1)
+    def _():
+        fine_halo.wait_send()
+        coarse_halo.wait_send()
+
+    first_out.wait()
+    second_out.wait()
+
+
+HALO_TIME = 0.4
+CROP_TIME = 0.62
+
+
+def per_device_by_chips(
+    grid, proposal_boxes, level_plan, fine_map, coarse_map, first_weight, second_weight, upstream
+):
+    nz, nx, ny, cores = grid
+    chips = nz * nx
+    band = lax.axis_index("tile")
+    core = lax.axis_index("dp") % cores
+    num_props = level_plan.shape[1]
+    capacity = num_props // ny
+    fine_tile, coarse = fine_map[0], coarse_map[0]
+    fine_rows, fine_cols, channels = fine_tile.shape
+    coarse_rows, coarse_cols = coarse.shape[:2]
+    share, h = first_weight.shape
+    feats = share * ny
+    bins = max(-(-((t + 1) * share) // 128) - t * share // 128 for t in range(ny))
+    lanes = bins * 128
+    hidden_size = upstream.shape[2]
+    depth = second_weight.shape[0] // cores
+    pair = cores * h
+
+    fields, levels = proposal_boxes[0], level_plan[0]
+    member = (fields[0] // (4 * fine_rows) == band).astype(jnp.int32)
+    rank = jnp.cumsum(member) - 1
+    slot = jnp.where(member == 1, rank, -1)
+    chosen = slot[None, :] == jnp.arange(capacity, dtype=jnp.int32)[:, None]
+    picks = chosen.astype(jnp.bfloat16)
+    up = jnp.dot(picks, upstream[0], preferred_element_type=jnp.float32).astype(jnp.bfloat16)
+    up_turned = lax.dot_general(
+        upstream[0], picks, (((0,), (1,)), ((), ())), preferred_element_type=jnp.float32
+    ).astype(jnp.bfloat16)
+    mine = chosen.astype(jnp.int32)
+    top, left, height, box_width = (
+        jnp.sum(mine * fields[f][None, :], axis=1) for f in range(4)
+    )
+    level = jnp.sum(mine * levels[None, :], axis=1)
+    is_fine = level == 0
+    stride = jnp.where(is_fine, 4, 8).astype(jnp.int32)
+    first_row = top // stride
+    band_rows = jnp.where(is_fine, fine_rows, coarse_rows)
+    local_row = jnp.clip(first_row - band * band_rows, 0, band_rows - 1)
+    first_col = jnp.minimum(left // stride, jnp.where(is_fine, fine_cols, coarse_cols) - WIN)
+    cells = jnp.stack(
+        [local_row + jnp.where(is_fine, 0, fine_rows + HALO), first_col], axis=0
+    ).astype(jnp.int32)
+    stride_float = stride.astype(jnp.float32)
+    geo = jnp.stack(
+        [
+            top.astype(jnp.float32) / stride_float - first_row.astype(jnp.float32),
+            height.astype(jnp.float32) / (7.0 * stride_float),
+            left.astype(jnp.float32) / stride_float - first_col.astype(jnp.float32),
+            box_width.astype(jnp.float32) / (7.0 * stride_float),
+        ],
+        axis=0,
+    )
+    second_sets = (
+        second_weight.T.reshape(h, depth // h, cores, h).transpose(2, 0, 1, 3).reshape(cores, h, depth)
+    )
+
+    low, f32 = jnp.bfloat16, jnp.float32
+    sizes = (nz, nx, ny)
+    sum_parts = cut(bins, SCATTER_SHARES)
+    slot_counts = [sum(slots_of(sizes, order)) for order in ORDERS]
+    rows_all = chips * h
+    batch = cores * capacity
+    q = chips * ny
+    dma = pltpu.SemaphoreType.DMA
+    anywhere = pl.BlockSpec(memory_space=pl.ANY)
+    smem = pl.BlockSpec(memory_space=pltpu.SMEM)
+    first, second = pl.pallas_call(
+        functools.partial(step_kernel, grid),
+        out_shape=(
+            jax.ShapeDtypeStruct((share, h), f32),
+            jax.ShapeDtypeStruct((cores, h, depth), f32),
+        ),
+        in_specs=[smem, smem] + [anywhere] * 6,
+        out_specs=(anywhere, anywhere),
+        scratch_shapes=[
+            pltpu.VMEM((lanes, h), low),
+            pltpu.VMEM((ny, rows_all, lanes), low),
+            pltpu.VMEM((ny, hidden_size, depth), low),
+            pltpu.VMEM((fine_rows + HALO, fine_cols, channels), low),
+            pltpu.VMEM((coarse_rows + HALO, coarse_cols, channels), low),
+            pltpu.VMEM((fine_rows + coarse_rows + 2 * HALO, fine_cols, channels), f32),
+            pltpu.VMEM((ROWS_PAD * GROUP, 128), f32),
+            pltpu.VMEM((batch, feats), low),
+            pltpu.VMEM((batch, hidden_size), low),
+            pltpu.VMEM((cores, hidden_size, capacity), low),
+            pltpu.VMEM((rows_all, batch), f32),
+            pltpu.VMEM((rows_all, batch), f32),
+            pltpu.VMEM((rows_all, batch), low),
+            pltpu.VMEM((rows_all, batch), low),
+            pltpu.VMEM((ny, rows_all, lanes), low),
+            pltpu.VMEM((ny, hidden_size, depth), low),
+            pltpu.VMEM((slot_counts[0], h, sum_parts[0][1] * 128), low),
+            pltpu.VMEM((slot_counts[1], h, sum_parts[1][1] * 128), low),
+            pltpu.VMEM((slot_counts[2], h, sum_parts[2][1] * 128), low),
+            pltpu.VMEM((slot_counts[3], pair, depth), low),
+            pltpu.VMEM((lanes, h), f32),
+            pltpu.VMEM((cores, h, depth), f32),
+            pltpu.VMEM((2, h, depth), low),
+            dma((8,)),
+            dma((4, q, 6)),
+            dma((4, q)),
+            dma((4, q)),
+            dma((4, max(slot_counts))),
+            dma((6,)),
+            dma((6,)),
+            dma((capacity // GROUP,)),
+            dma((capacity // GROUP,)),
+        ],
+        compiler_params=pltpu.CompilerParams(
+            collective_id=0, has_side_effects=True, vmem_limit_bytes=64000 * 1024
+        ),
+        name="step",
+    )(cells, geo, first_weight, second_sets, up, up_turned, fine_tile, coarse)
+    turned = second.reshape(cores, h, depth // h, h).transpose(2, 0, 3, 1)
+    return (first, turned.reshape(cores * depth, h))
+
+
 def solution(mesh):
     placed = (
         P("dp", None, None),
@@ -254,8 +1076,13 @@
         P("tile", "dp"),
         P("dp", None, None),
     )
+    grid = chip_grid(mesh)
+    tiles = mesh.shape["tile"]
+    body = per_device_by_bands
+    if grid is not None and tiles == 2 and grid[1] <= 2 and grid[2] == 2:
+        body = functools.partial(per_device_by_chips, (grid[0], grid[1], tiles, grid[2]))
     return jax.shard_map(
-        per_device,
+        body,
         mesh=mesh,
         in_specs=placed,
         out_specs=(P("tile", "dp"), P("tile", "dp")),

time: 264 us -> 178 us (0.67)
  waiting for transfers between devices: 174 us -> 0 us
  Pallas kernels: 13.2 us -> 162 us
  matrix products: 24 us -> 0.55 us
  other arithmetic: 21.3 us -> 4.72 us
  between operations: 14.4 us -> 0.76 us
  local copies, waits for them, and re-layouts: 14.1 us -> 9.1 us
    pallas_call x1, Pallas kernels: 13.2 us -> 162 us  [per_device_by_chips(): pl.pallas_call(functools.partial(step_kernel, grid), out_shape=(jax.Shape...]
    reduce_scatter x1 -> x0, waiting for transfers between devices: 93.3 us -> none  [per_device(): lax.psum_scatter(jnp.concatenate([first_part, second_part], axis=1), 'dp'...]
    ppermute x4 -> x0, waiting for transfers between devices: 80.9 us -> none  [the longest x3 56.4 us: from_ahead(): lax.ppermute(block, axis, [(i, (i - distance) % size) for i in range(size)])]
    dot_general x5 -> x1, matrix products: 24 us -> 0.55 us  [per_device_by_chips(): jnp.dot(picks, upstream[0], preferred_element_type=jnp.float32)]
    concatenate x4 -> x0, other arithmetic: 18.2 us -> none  [the longest x1 8.77 us: per_device(): jnp.concatenate([fine_tile, below_rows[:, :fine_cols], jnp.pad(coarse, si...]
    dynamic_update_slice x1 -> x0, local copies, waits for them, and re-layouts: 4.99 us -> none  [per_device(): lax.dynamic_update_slice(jnp.zeros((first_weight.shape[1], lanes), jnp.bf...]
    unnamed x18 -> x10, local copies, waits for them, and re-layouts: 1.4 us -> 4.82 us
    slice x9 -> x1, local copies, waits for them, and re-layouts: 3.36 us -> 0.07 us  [the longest x1 1.22 us: per_device(): below_rows[:, :fine_cols]]
  transfers between devices with their start and end apart: 6 -> 0, of which waited for: 5 -> 0; matrix products, arithmetic and copies ran while one was open for 8% -> 0% of each run, Pallas kernels for 5% -> 0%
where the time goes in v1:
time: 178 us
  Pallas kernels  162 us (91%)
  local copies, waits for them, and re-layouts  9.1 us (5%)
  other arithmetic  4.72 us (3%)
    pallas_call x1, Pallas kernels, per_device_by_chips(): pl.pallas_call(functools.partial(step_kernel, grid), out_shape=(jax.Shape...  162 us
    unnamed x10, local copies, waits for them, and re-layouts  4.82 us

profile of v1, /device:TPU:0, one launch (start us, length us, event | category | flops | bytes accessed | tf_op | source)
XLA Modules:
  0.0 177.5 jit_solution(4998908498045875190)
XLA Ops:
  0.6 0.0 copy-start
  0.6 0.0 copy-start.2
  0.7 0.8 and_reduce_fusion
  1.5 0.9 fusion.11
  2.4 0.3 reduce-window.9
  2.7 0.1 slice.25
  2.8 0.1 slice_reduce_fusion
  2.9 0.1 bitcast_select_fusion
  3.0 1.1 select_reduce_fusion.1
  4.1 0.1 compare_and_fusion.1
  4.2 0.1 select_divide_fusion.1
  4.4 0.6 pad_maximum_fusion.geo_ref
  5.0 0.6 pad_add_fusion.cells_ref
  5.6 1.0 reshape.311
  6.6 0.8 reshape.312.w2_ref
  7.4 0.0 copy-done
  7.4 0.5 convolution_convert_fusion
  8.0 0.0 copy-start.1
  8.0 0.8 copy-done.1
  8.8 1.0 copy.24.up_ref
  9.8 0.0 copy-done.2
  9.8 1.2 copy.23.w1_ref
  11.0 162.4 %step.1 = (f32[3136,64]{1,0:T(8,128)}, f32[2,64,256]{2,1,0:T(8,128)}) custom-call(s32[2,256]{1,0:T(2,128)} %pad_add_fusion.cells_ref, f32[4,256]{1,0:T(4,128)} %pad_maximum_fusion.geo_ref, bf16[3136,64]{1,0:T(8,128)(2,1)} %copy.23.w1_ref, bf16[2,64,256]{2,1,0:T(8,128)(2,1)} %reshape.312.w2_ref, bf16[256,1024]{1,0:T(8,128)(2,1)} %copy.24.up_ref, ...), custom_call_target="tpu_custom_call" | custom-call | tf_op jit(solution)/shard_map/step/pallas_call | solution.py:1018
  173.4 0.0 copy-start.3
  173.4 2.8 %copy.26 = f32[3136,64]{0,1:T(8,128)} copy(f32[3136,64]{1,0:T(8,128)} %get-tuple-element.10) | data formatting | bytes 1605632
  176.2 0.0 copy-done.3
  176.2 0.2 reshape.313
  176.4 0.2 copy.25
  176.6 0.9 reshape.314
  (7 shorter events, 0.1 us)
Async XLA Ops:
  0.6 6.8 %copy-start = (bf16[1,512,1024]{2,1,0:T(8,128)(2,1)S(1)}, bf16[1,512,1024]{2,1,0:T(8,128)(2,1)}, u32[]{:S(2)}) copy-start(bf16[1,512,1024]{2,1,0:T(8,128)(2,1)} %param.13) | copy-start | bytes 3145732
  0.6 9.1 %copy-start.2 = (bf16[3136,64]{0,1:T(8,128)(2,1)S(1)}, bf16[3136,64]{0,1:T(8,128)(2,1)}, u32[]{:S(2)}) copy-start(bf16[3136,64]{0,1:T(8,128)(2,1)} %param.11) | copy-start | bytes 1204228
  8.0 0.8 copy-start.1
  173.4 2.8 %copy-start.3 = (f32[2,64,256]{2,1,0:T(8,128)S(1)}, f32[2,64,256]{2,1,0:T(8,128)}, u32[]{:S(2)}) copy-start(f32[2,64,256]{2,1,0:T(8,128)} %get-tuple-element.5) | copy-start | bytes 393220

commit v2 on v0

--- a/solution.py
+++ b/solution.py
@@ -104,7 +104,7 @@
     )(cells, geo, maps)
 
 
-def per_device(
+def per_device_by_bands(
     proposal_boxes, level_plan, fine_map, coarse_map, first_weight, second_weight, upstream
 ):
     tile_count = lax.axis_size("tile")
@@ -244,6 +244,877 @@
     return (first_grad, second_grad)
 
 
+MESH = pl.DeviceIdType.MESH
+REACH = 15
+HALO = REACH - 1
+NT = (((1,), (1,)), ((), ()))
+NN = (((1,), (0,)), ((), ()))
+
+
+def chip_grid(mesh):
+    chips = [getattr(device, "coords", None) for device in mesh.devices[:, 0]]
+    if chips[0] is None:
+        return None
+    cores = sum(1 for c in chips if tuple(c) == tuple(chips[0]))
+    chips = [tuple(c) for c in chips[::cores]]
+    if len(chips) == 1:
+        return (1, 1, cores)
+    axis = [a != b for a, b in zip(chips[0], chips[1])].index(True)
+    fast = 1
+    while fast < len(chips) and all(
+        a == b or i == axis for i, (a, b) in enumerate(zip(chips[0], chips[fast]))
+    ):
+        fast += 1
+    return (len(chips) // fast, fast, cores)
+
+
+def offsets(size):
+    if size == 1:
+        return [0]
+    if size == 2:
+        return [0, 1]
+    return [0] + [s * d for d in range(1, size) for s in (-1, 1)]
+
+
+def steps_of(size):
+    return {1: [], 2: [1]}.get(size, [-1, 1])
+
+
+def moved(position, size, rel):
+    if rel == 0 or size == 1:
+        return position
+    return 1 - position if size == 2 else position + rel
+
+
+def last_axis(order, rel):
+    used = [j for j in range(3) if rel[order[j]]]
+    return used[-1] if used else -1
+
+
+def onward(sizes, order, rel):
+    last = last_axis(order, rel)
+    hops = []
+    if last >= 0:
+        axis = order[last]
+        if sizes[axis] > 2 and abs(rel[axis]) < sizes[axis] - 1:
+            hops.append((last, axis, -1 if rel[axis] > 0 else 1))
+    for j in range(last + 1, 3):
+        hops.extend((j, order[j], step) for step in steps_of(sizes[order[j]]))
+    return hops
+
+
+def arrival_order(sizes, routes, extra):
+    import heapq
+    import itertools
+
+    places = list(itertools.product(*(range(n) for n in sizes)))
+    queue, waiting, busy = [], {}, set()
+    seen, tick = {}, itertools.count()
+
+    def start(link, now):
+        if link not in busy and waiting.get(link):
+            busy.add(link)
+            load, arrival = waiting[link].pop(0)
+            heapq.heappush(queue, (now + load, next(tick), link, arrival))
+
+    def arrive(place, route, rel, now):
+        seen.setdefault((route, rel), []).append(now)
+        for _, axis, step in onward(sizes, routes[route][0], rel):
+            target = list(place)
+            target[axis] = moved(place[axis], sizes[axis], step)
+            if not 0 <= target[axis] < sizes[axis]:
+                continue
+            there = list(rel)
+            there[axis] = rel[axis] - step if sizes[axis] > 2 else 1
+            link = (place, axis, step)
+            waiting.setdefault(link, []).append(
+                (routes[route][1], (tuple(target), route, tuple(there)))
+            )
+            start(link, now)
+
+    first = {}
+    for place in places:
+        for route in extra[1]:
+            arrive(place, route, (0, 0, 0), 0.0)
+        if extra[0] and place[2] == 1:
+            waiting.setdefault((place, 2, 1), []).append((extra[0], None))
+            start((place, 2, 1), 0.0)
+        for route in range(len(routes)):
+            if route not in extra[1]:
+                arrive(place, route, (0, 0, 0), 0.0)
+    end = 0.0
+    while queue:
+        now, _, link, arrival = heapq.heappop(queue)
+        end = now
+        busy.discard(link)
+        if arrival is not None:
+            arrive(*arrival, now)
+        start(link, now)
+    key = {event: sum(t) / len(t) for event, t in seen.items()}
+    for _ in range(sum(sizes)):
+        for (route, rel) in list(key):
+            for _, axis, step in onward(sizes, routes[route][0], rel):
+                there = list(rel)
+                there[axis] = rel[axis] - step if sizes[axis] > 2 else 1
+                event = (route, tuple(there))
+                if event in key:
+                    key[event] = max(key[event], key[(route, rel)] + 1e-3)
+    return sorted(key, key=lambda e: (key[e], e)), key, end
+
+
+def slots_of(sizes, order):
+    counts, before = [], 1
+    for j in range(3):
+        n = sizes[order[j]]
+        counts.append(before * (2 * n if n > 2 else 1))
+        before *= n
+    return counts
+
+
+def when(conds, body):
+    if not conds:
+        body()
+        return
+    total = conds[0]
+    for cond in conds[1:]:
+        total = jnp.logical_and(total, cond)
+    pl.when(total)(body)
+
+
+class Routes:
+    def __init__(self, sizes, position, core, cores, orders):
+        self.sizes, self.position = sizes, position
+        self.core, self.cores = core, cores
+        self.orders = orders
+        self.slot_counts = [slots_of(sizes, order) for order in orders]
+        self.slot_base = [sum(sum(c) for c in self.slot_counts[:i]) for i in range(len(orders))]
+
+    def inside(self, axis, rel):
+        if rel == 0 or self.sizes[axis] <= 2:
+            return []
+        p = self.position[axis]
+        return [p < self.sizes[axis] - rel] if rel > 0 else [p >= -rel]
+
+    def valid(self, rel):
+        return sum((self.inside(axis, rel[axis]) for axis in range(3)), [])
+
+    def at(self, rel):
+        return [moved(self.position[a], self.sizes[a], rel[a]) for a in range(3)]
+
+    def device(self, axis, step):
+        there = list(self.position)
+        there[axis] = moved(there[axis], self.sizes[axis], step)
+        return ((there[0] * self.sizes[1] + there[1]) * self.cores + self.core, there[2])
+
+    def back_step(self, order, rel):
+        axis = order[last_axis(order, rel)]
+        return axis, (1 if self.sizes[axis] == 2 or rel[axis] > 0 else -1)
+
+    def number(self, place):
+        return (place[0] * self.sizes[1] + place[1]) * self.sizes[2] + place[2]
+
+    def direction(self, axis, step):
+        return 2 * axis + (1 if step > 0 else 0)
+
+    def drain(self, route, whole, unit, sems):
+        order, before = self.orders[route], 1
+        for axis in order:
+            n, p = self.sizes[axis], self.position[axis]
+            for step in steps_of(n):
+                for at in range(n) if n > 2 else [0]:
+                    sent = before * ((at + 1 if step > 0 else n - at) if n > 2 else 1)
+                    if n > 2 and not 0 <= at + step < n:
+                        continue
+
+                    def wait(axis=axis, step=step, sent=sent):
+                        part = whole(sent * unit)
+                        pltpu.make_async_copy(
+                            part, part, sems.at[route, self.direction(axis, step)]
+                        ).wait()
+
+                    when([p == at] if n > 2 else [], wait)
+            before *= n
+
+    def gather(self, route, rel, ref_of, send_sems, recv_sems):
+        order = self.orders[route]
+
+        def body():
+            place = self.at(rel)
+            ref = ref_of(place)
+            q = self.number(place)
+
+            def hop(axis, step):
+                return pltpu.make_async_remote_copy(
+                    src_ref=ref,
+                    dst_ref=ref,
+                    send_sem=send_sems.at[route, self.direction(axis, step)],
+                    recv_sem=recv_sems.at[route, q],
+                    device_id=self.device(axis, step),
+                    device_id_type=MESH,
+                )
+
+            if last_axis(order, rel) >= 0:
+                hop(*self.back_step(order, rel)).wait_recv()
+            for _, axis, step in onward(self.sizes, order, rel):
+                copy = hop(axis, step)
+                when(self.inside(axis, step), copy.start)
+
+        when(self.valid(rel), body)
+
+    def slot(self, route, phase, side, place):
+        order, counts = self.orders[route], self.slot_counts[route]
+        index = 0
+        for j in range(phase):
+            index = index * self.sizes[order[j]] + place[order[j]]
+        n = self.sizes[order[phase]]
+        if n > 2:
+            index = (index * n + place[order[phase]]) * 2 + (1 if side > 0 else 0)
+        return sum(counts[:phase]) + index
+
+    def scatter(self, route, rel, ref_of, slots, add, send_sems, recv_sems):
+        order = self.orders[route]
+
+        def body():
+            place = self.at(rel)
+            ref = ref_of(place)
+            base = self.slot_base[route]
+            for phase, axis, step in onward(self.sizes, order, rel):
+                slot = self.slot(route, phase, step, place)
+
+                def take(axis=axis, step=step, slot=slot):
+                    pltpu.make_async_remote_copy(
+                        src_ref=ref,
+                        dst_ref=slots.at[slot],
+                        send_sem=send_sems.at[route],
+                        recv_sem=recv_sems.at[base + slot],
+                        device_id=self.device(axis, step),
+                        device_id_type=MESH,
+                    ).wait_recv()
+                    add(ref, slots.at[slot])
+
+                when(self.inside(axis, step), take)
+            phase = last_axis(order, rel)
+            if phase >= 0:
+                axis, step = self.back_step(order, rel)
+                slot = self.slot(route, phase, 1 if self.sizes[axis] == 2 else -step, place)
+                pltpu.make_async_remote_copy(
+                    src_ref=ref,
+                    dst_ref=slots.at[slot],
+                    send_sem=send_sems.at[route],
+                    recv_sem=recv_sems.at[base + slot],
+                    device_id=self.device(axis, step),
+                    device_id_type=MESH,
+                ).start()
+
+        when(self.valid(rel), body)
+
+
+def cut(bins, shares):
+    edges = [0]
+    for i in range(1, len(shares) + 1):
+        edges.append(round(bins * sum(shares[:i]) / sum(shares)))
+    return [(a, b - a) for a, b in zip(edges, edges[1:])]
+
+
+GATHER_ORDERS = ((2, 0, 1), (0, 1, 2), (1, 2, 0), (2, 0, 1))
+GATHER_SHARES = (10, 11, 4)
+SCATTER_ORDERS = ((2, 0, 1), (0, 1, 2), (1, 2, 0), (2, 0, 1))
+SCATTER_SHARES = (6, 16, 3)
+HALO_AFTER = 4
+EARLY, DURING, LAST = 18, 30, 8
+GATHER_CODES = {
+    (4, 2, 2): (
+        84, 0, 56, 28, 1, 85, 58, 88, 4, 8, 57, 89, 29, 9, 36, 92, 32, 5, 86, 40, 64, 93, 97,
+        16, 59, 12, 30, 38, 44, 65, 100, 37, 90, 24, 87, 17, 48, 13, 10, 61, 101, 63, 50, 34,
+        18, 7, 66, 20, 42, 73, 96, 3, 2, 62, 6, 49, 26, 31, 60, 52, 39, 45, 104, 33, 95, 46, 69,
+        25, 108, 21, 67, 91, 14, 68, 105, 109, 106, 41, 77, 54, 82, 76, 74, 71, 72, 53, 23, 94,
+        75, 11, 111, 22, 70, 102, 19, 81, 107, 110, 27, 35, 99, 47, 98, 103, 15, 80, 79, 51, 78,
+        43, 55, 83
+    ),
+}
+SCATTER_CODES = {
+    (4, 2, 2): (
+        111, 26, 78, 23, 94, 51, 47, 106, 43, 35, 55, 99, 82, 37, 22, 80, 107, 110, 77, 81, 103,
+        79, 18, 74, 27, 53, 109, 98, 11, 69, 73, 76, 83, 45, 24, 108, 7, 102, 101, 87, 61, 19,
+        90, 95, 49, 75, 54, 66, 68, 25, 15, 100, 71, 63, 39, 104, 20, 70, 50, 72, 105, 10, 16,
+        14, 91, 46, 65, 42, 41, 17, 2, 67, 92, 97, 31, 64, 33, 93, 29, 88, 21, 96, 6, 3, 52, 34,
+        13, 48, 89, 9, 5, 12, 62, 40, 4, 38, 85, 60, 44, 8, 59, 1, 30, 32, 36, 58, 57, 86, 0,
+        56, 28, 84
+    ),
+}
+
+
+def unpack(codes, sizes):
+    spans = [offsets(n) for n in sizes]
+    events = []
+    for code in codes:
+        code, k = divmod(code, len(spans[2]))
+        code, j = divmod(code, len(spans[1]))
+        route, i = divmod(code, len(spans[0]))
+        events.append((route, (spans[0][i], spans[1][j], spans[2][k])))
+    return events
+
+
+def step_kernel(grid, *refs):
+    fields_ref, levels_ref, w1_ref, w2_ref, up_ref, fine_ref, coarse_ref = refs[:7]
+    first_ref, second_ref = refs[7:9]
+    (
+        w_in,
+        w2_in,
+        w2_sets,
+        wbuf,
+        w2buf,
+        fine_low,
+        coarse_low,
+        wide,
+        stage,
+        crops,
+        up_all,
+        upb,
+        uptb,
+        back,
+        hidden,
+        acts,
+        pres,
+        grads,
+        seconds,
+        out_first,
+        out_second,
+        swap,
+        cells_v,
+        geo_v,
+        cells_ref,
+        geo_ref,
+        local_sems,
+        send_sems,
+        recv_sems,
+        sum_send_sems,
+        sum_recv_sems,
+        core_send,
+        core_recv,
+    ) = refs[9:42]
+    slot_refs = refs[42:]
+    nz, nx, ny, cores = grid
+    sizes = (nz, nx, ny)
+    dp = lax.axis_index("dp")
+    y = lax.axis_index("tile")
+    core = dp % cores
+    chip = dp // cores
+    x = chip % nx
+    z = chip // nx
+    position = (z, x, y)
+    other = 1 - core
+    partner = (chip * cores + other, y)
+    ways_in = Routes(sizes, position, core, cores, GATHER_ORDERS)
+    ways_out = Routes(sizes, position, core, cores, SCATTER_ORDERS)
+    h, share = w1_ref.shape
+    lanes = wbuf.shape[1]
+    bins = lanes // 128
+    all_rows = nz * nx * h
+    fine_rows, fine_cols, _ = fine_ref.shape
+    coarse_rows, coarse_cols, _ = coarse_ref.shape
+    batch, feats = crops.shape
+    capacity = batch // cores
+    depth = w2buf.shape[1]
+    hidden_size = up_ref.shape[1]
+    pair = cores * h
+    starts = [min(t * share // 128, feats // 128 - bins) for t in range(ny)]
+    shift = share - 128 * starts[1]
+    parts_in = cut(bins, GATHER_SHARES)
+    parts_out = cut(bins, SCATTER_SHARES)
+    f32, low = jnp.float32, jnp.bfloat16
+
+    barrier = pltpu.get_barrier_semaphore()
+    pl.semaphore_signal(barrier, inc=1, device_id=partner, device_id_type=MESH)
+    peers = 1
+    for axis in range(3):
+        for step in steps_of(sizes[axis]):
+
+            def greet(axis=axis, step=step):
+                pl.semaphore_signal(
+                    barrier, inc=1, device_id=ways_in.device(axis, step), device_id_type=MESH
+                )
+
+            near = ways_in.inside(axis, step)
+            when(near, greet)
+            peers = peers + (near[0].astype(jnp.int32) if near else 1)
+
+    def rows(start, size):
+        return pl.ds(pl.multiple_of(start, size), size)
+
+    def local(src, dst, i):
+        copy = pltpu.make_async_copy(src, dst, local_sems.at[i])
+        copy.start()
+        return copy
+
+    def remote(src, dst, i, device):
+        return pltpu.make_async_remote_copy(
+            src_ref=src,
+            dst_ref=dst,
+            send_sem=core_send.at[i],
+            recv_sem=core_recv.at[i],
+            device_id=device,
+            device_id_type=MESH,
+        )
+
+    w_copy = local(w1_ref, w_in, 0)
+    w2_copy = local(w2_ref, w2_in, 1)
+    fine_copy = local(fine_ref, fine_low.at[pl.ds(0, fine_rows)], 2)
+    coarse_copy = local(coarse_ref, coarse_low.at[pl.ds(0, coarse_rows)], 3)
+    up_copy = local(up_ref, up_all, 4)
+    halves = lax.broadcasted_iota(jnp.int32, (h, 128), 1)
+
+    w_copy.wait()
+    own_rows = pl.ds(pl.multiple_of(y * all_rows + chip * h, h), h)
+    before = jnp.zeros((h, 128), f32)
+    for i in range(bins):
+        width = min(128, share - 128 * i)
+        now = w_in[:, 128 * i : 128 * i + width].astype(f32)
+        if width < 128:
+            now = jnp.concatenate([now, jnp.zeros((h, 128 - width), f32)], axis=1)
+        turned = pltpu.roll(now, shift, axis=1) if shift else now
+        late = jnp.where(halves < shift, before, turned)
+        before = turned
+        wbuf[own_rows, 128 * i : 128 * (i + 1)] = jnp.where(y == 0, now, late).astype(low)
+
+    w2_copy.wait()
+    for m in range(depth // 128):
+        a = w2_in[:, 256 * m : 256 * m + 128].astype(f32)
+        b = w2_in[:, 256 * m + 128 : 256 * m + 256].astype(f32)
+        at = slice(128 * m, 128 * (m + 1))
+        w2_sets[0, :, at] = jnp.where(halves < h, a, pltpu.roll(b, h, axis=1)).astype(low)
+        w2_sets[1, :, at] = jnp.where(halves < h, pltpu.roll(a, h, axis=1), b).astype(low)
+    w2_rows = pl.ds(pl.multiple_of(y * hidden_size + chip * pair + core * h, h), h)
+    w2buf[w2_rows, :] = w2_sets[core]
+
+    pl.semaphore_wait(barrier, peers)
+    w2_swap = remote(w2_sets.at[other], w2buf.at[w2_rows, :], 0, partner)
+
+    last_in = len(GATHER_SHARES)
+    last_out = len(SCATTER_SHARES)
+    loads_in = [
+        (order, parts_in[i][1] if i < last_in else depth * pair // (h * 128))
+        for i, order in enumerate(GATHER_ORDERS)
+    ]
+    loads_out = [
+        (order, parts_out[i][1] if i < last_out else depth * pair // (h * 128))
+        for i, order in enumerate(SCATTER_ORDERS)
+    ]
+    halo_load = HALO * (fine_cols + coarse_cols) // h
+    if sizes in GATHER_CODES:
+        events = unpack(GATHER_CODES[sizes], sizes)
+        sum_events = unpack(SCATTER_CODES[sizes], sizes)
+    else:
+        events = arrival_order(sizes, loads_in, (halo_load, (0,)))[0]
+        sum_events = arrival_order(sizes, loads_out, (0, ()))[0][::-1]
+
+    def gather_ref(route):
+        if route == last_in:
+            return lambda q: w2buf.at[
+                rows(q[2] * hidden_size + (q[0] * nx + q[1]) * pair, pair), :
+            ]
+        first, count = parts_in[route]
+        return lambda q: wbuf.at[
+            rows(q[2] * all_rows + (q[0] * nx + q[1]) * h, h), pl.ds(first * 128, count * 128)
+        ]
+
+    def gather(event):
+        route, rel = event
+        ways_in.gather(route, rel, gather_ref(route), send_sems, recv_sems)
+
+    w2_swap.start()
+    below = ways_in.device(2, 1)
+    fine_halo = remote(
+        fine_ref.at[pl.ds(0, HALO)], fine_low.at[pl.ds(fine_rows, HALO)], 1, below
+    )
+    coarse_halo = remote(
+        coarse_ref.at[pl.ds(0, HALO)], coarse_low.at[pl.ds(coarse_rows, HALO)], 2, below
+    )
+    own = [e for e in events if e[1] == (0, 0, 0)]
+    todo = [e for e in events if e[1] != (0, 0, 0)]
+    for n, event in enumerate(own):
+        if event[0] == last_in:
+            w2_swap.wait()
+        gather(event)
+        if n + 1 == HALO_AFTER:
+
+            @pl.when(y == 1)
+            def _():
+                fine_halo.start()
+                coarse_halo.start()
+
+    member = jnp.logical_and(
+        fields_ref[0:1, :] >= y * (4 * fine_rows), fields_ref[0:1, :] < (y + 1) * (4 * fine_rows)
+    )
+    props = fields_ref.shape[1]
+    ones = jnp.broadcast_to(jnp.where(member, 1.0, 0.0), (8, props)).astype(low)
+    upto = lax.broadcasted_iota(jnp.int32, (props, props), 0) <= lax.broadcasted_iota(
+        jnp.int32, (props, props), 1
+    )
+    rank = jnp.dot(ones, jnp.where(upto, 1.0, 0.0).astype(low), preferred_element_type=f32)
+    slot = jnp.where(member, rank[0:1, :] - 1.0, -1.0)
+    slot_ids = lax.broadcasted_iota(jnp.int32, (capacity, props), 0).astype(f32)
+    picks = jnp.where(slot == slot_ids, 1.0, 0.0).astype(low)
+
+    def pick(ints):
+        return lax.dot_general(
+            ints.astype(f32).astype(low), picks, NT, preferred_element_type=f32
+        )
+
+    boxes = jnp.concatenate([fields_ref[...], fields_ref[...]], axis=0)
+    values = 8.0 * pick(boxes >> 3) + pick(boxes & 7)
+    level = pick(jnp.broadcast_to(levels_ref[...], (8, props)))[0:1, :]
+    top, left, height, box_width = (values[i : i + 1, :] for i in range(4))
+    is_fine = level < 0.5
+    inverse = jnp.where(is_fine, 0.25, 0.125)
+    span = jnp.where(is_fine, 28.0, 56.0)
+    first_row = jnp.floor(top * inverse)
+    band_rows = jnp.where(is_fine, 1.0 * fine_rows, 1.0 * coarse_rows)
+    local_row = jnp.clip(first_row - y.astype(f32) * band_rows, 0.0, band_rows - 1.0)
+    first_col = jnp.minimum(
+        jnp.floor(left * inverse), jnp.where(is_fine, 1.0 * fine_cols, 1.0 * coarse_cols) - WIN
+    )
+    cells_v[0:1, :] = (local_row + jnp.where(is_fine, 0.0, 1.0 * (fine_rows + HALO))).astype(
+        jnp.int32
+    )
+    cells_v[1:2, :] = first_col.astype(jnp.int32)
+    geo_v[0:1, :] = top * inverse - first_row
+    geo_v[1:2, :] = height / span
+    geo_v[2:3, :] = left * inverse - first_col
+    geo_v[3:4, :] = box_width / span
+    up_copy.wait()
+    half = rows(core * capacity, capacity)
+    upb[half, :] = jnp.dot(picks, up_all[...], preferred_element_type=f32).astype(low)
+    cells_copy = local(cells_v, cells_ref, 5)
+    geo_copy = local(geo_v, geo_ref, 6)
+
+    coarse_base = fine_rows + HALO
+
+    def widen(source, first, count, base, cols):
+        def one(r, carry):
+            wide[base + r, 0:cols, :] = source[r].astype(f32)
+            return carry
+
+        lax.fori_loop(first, first + count, one, 0)
+
+    fine_copy.wait()
+    coarse_copy.wait()
+    widen(fine_low, 0, fine_rows, 0, fine_cols)
+    widen(coarse_low, 0, coarse_rows, coarse_base, coarse_cols)
+    up_swap = remote(upb.at[half, :], upb.at[half, :], 3, partner)
+    up_swap.start()
+
+    for event in todo[:EARLY]:
+        gather(event)
+
+    @pl.when(y == 0)
+    def _():
+        fine_halo.wait_recv()
+        coarse_halo.wait_recv()
+        widen(fine_low, fine_rows, HALO, 0, fine_cols)
+        widen(coarse_low, coarse_rows, HALO, coarse_base, coarse_cols)
+
+    @pl.when(y == 1)
+    def _():
+        def clear(r, carry):
+            wide[r] = jnp.zeros(wide.shape[1:], f32)
+            return carry
+
+        lax.fori_loop(fine_rows, fine_rows + HALO, clear, 0)
+        lax.fori_loop(coarse_base + coarse_rows, coarse_base + coarse_rows + HALO, clear, 0)
+
+    cells_copy.wait()
+    geo_copy.wait()
+
+    groups = capacity // GROUP
+    during = todo[EARLY : EARLY + DURING]
+    todo = todo[EARLY + DURING :]
+    shape = (ROWS_PAD, REACH * WIN)
+    k = lax.broadcasted_iota(jnp.int32, shape, 0).astype(f32)
+    i_bin = jnp.floor((k + 0.5) * (1.0 / BINS))
+    j_bin = k - BINS * i_bin
+    i_mid = i_bin + 0.5
+    j_mid = j_bin + 0.5
+    lane = lax.broadcasted_iota(jnp.int32, shape, 1)
+    r_cell = (lane >> 4).astype(f32)
+    q_cell = (lane & 15).astype(f32)
+
+    def crop_copy(first, count):
+        crop_rows = pl.ds(pl.multiple_of(core * capacity + first, GROUP), count)
+        return remote(crops.at[crop_rows, :], crops.at[crop_rows, :], 4, partner)
+
+    def crop_group(g, carry):
+        for n, event in enumerate(during):
+            pl.when(g == n * groups // len(during))(functools.partial(gather, event))
+        for p in range(GROUP):
+            n = g * GROUP + p
+            row = jnp.clip(cells_ref[0, n], 0, wide.shape[0] - REACH)
+            col = jnp.clip(cells_ref[1, n], 0, fine_cols - WIN)
+            row_w = jnp.maximum(0.0, 1.0 - jnp.abs(i_mid * geo_ref[1, n] + geo_ref[0, n] - r_cell))
+            col_w = jnp.maximum(0.0, 1.0 - jnp.abs(j_mid * geo_ref[3, n] + geo_ref[2, n] - q_cell))
+            weights = (row_w * col_w).astype(low)
+            window = jnp.concatenate(
+                [wide[row + r, pl.ds(col, WIN), :] for r in range(REACH)], axis=0
+            ).astype(low)
+            crop = jnp.dot(weights, window, preferred_element_type=f32)
+            stage[pl.ds(p, ROWS_PAD, stride=GROUP), :] = crop
+        group_rows = rows(core * capacity + g * GROUP, GROUP)
+        for m in range(feats // 128):
+            crops[group_rows, m * 128 : (m + 1) * 128] = stage[
+                m * GROUP : (m + 1) * GROUP, :
+            ].astype(low)
+
+        @pl.when(g > 0)
+        def _():
+            crop_copy((g - 1) * GROUP, GROUP).start()
+
+        return carry
+
+    lax.fori_loop(0, groups, crop_group, 0)
+    crop_copy((groups - 1) * GROUP, GROUP).start()
+
+    for event in todo[:-LAST]:
+        gather(event)
+    up_swap.wait()
+
+    def turn_up(i, carry):
+        at = rows(i * 128, 128)
+        uptb[at, :] = upb[:, at].astype(f32).T.astype(low)
+        return carry
+
+    lax.fori_loop(0, hidden_size // 128, turn_up, 0)
+    for event in todo[-LAST:]:
+        gather(event)
+    for t in range(ny):
+        part = jnp.dot(
+            upb[...], w2buf[t * hidden_size : (t + 1) * hidden_size, :], preferred_element_type=f32
+        )
+        back[t * depth : (t + 1) * depth, :] = part.T
+    crop_copy(0, capacity).wait()
+
+    chunk = 640 if lanes % 640 == 0 else 128
+    hidden[...] = jnp.zeros_like(hidden)
+    for t in range(ny):
+
+        def hide(i, carry, t=t):
+            at = pl.multiple_of(i * chunk, 128)
+            from_at = pl.multiple_of(starts[t] * 128 + i * chunk, 128)
+            hidden[...] += lax.dot_general(
+                wbuf[t * all_rows : (t + 1) * all_rows, pl.ds(at, chunk)],
+                crops[:, pl.ds(from_at, chunk)],
+                NT,
+                preferred_element_type=f32,
+            )
+            return carry
+
+        lax.fori_loop(0, lanes // chunk, hide, 0)
+
+    def gelu(i, carry):
+        at = rows(i * 32, 32)
+        value, slope = gelu_parts(hidden[at, :])
+        acts[at, :] = value.astype(low)
+        pres[at, :] = (back[at, :] * slope).astype(low)
+        return carry
+
+    lax.fori_loop(0, hidden.shape[0] // 32, gelu, 0)
+
+    def sum_ref(route):
+        if route == last_out:
+            return lambda q: seconds.at[
+                rows(q[2] * hidden_size + (q[0] * nx + q[1]) * pair, pair), :
+            ]
+        first, count = parts_out[route]
+        return lambda q: grads.at[
+            rows(q[2] * all_rows + (q[0] * nx + q[1]) * h, h), pl.ds(first * 128, count * 128)
+        ]
+
+    def add(ref, more):
+        def one(i, carry):
+            at = rows(i * 16, 16)
+            ref[at, :] = (ref[at, :].astype(f32) + more[at, :].astype(f32)).astype(low)
+            return carry
+
+        lax.fori_loop(0, ref.shape[0] // 16, one, 0)
+
+    def make_grads(t, part):
+        first, count = parts_out[part]
+        step = max(c for c in range(1, 7) if count % c == 0)
+
+        def one(i, carry):
+            at = pl.multiple_of((first + i * step) * 128, 128)
+            from_at = pl.multiple_of((starts[0] + t * (starts[1] - starts[0])) * 128 + at, 128)
+            grads[rows(t * all_rows, all_rows), pl.ds(at, step * 128)] = jnp.dot(
+                pres[...], crops[:, pl.ds(from_at, step * 128)], preferred_element_type=f32
+            ).astype(low)
+            return carry
+
+        lax.fori_loop(0, count // step, one, 0)
+
+    def make_seconds():
+        for t in range(ny):
+            seconds[t * hidden_size : (t + 1) * hidden_size, :] = lax.dot_general(
+                uptb[...], acts[t * depth : (t + 1) * depth, :], NT, preferred_element_type=f32
+            ).astype(low)
+
+    made = set()
+    for route, rel in sum_events:
+        need = (route, rel[2] if route < last_out else 0)
+        if need not in made:
+            made.add(need)
+            if route == last_out:
+                make_seconds()
+            else:
+                make_grads(y if rel[2] == 0 else 1 - y, route)
+        ways_out.scatter(
+            route, rel, sum_ref(route), slot_refs[route], add, sum_send_sems, sum_recv_sems
+        )
+
+    own_second = y * hidden_size + chip * pair
+    swap[0] = seconds[pl.ds(pl.multiple_of(own_second + other * h, h), h), :]
+    second_swap = remote(swap.at[0], swap.at[1], 5, partner)
+    second_swap.start()
+    tile = grads[own_rows, 0:128].astype(f32)
+    back_shift = (128 - shift) % 128
+    now_turned = pltpu.roll(tile, back_shift, axis=1)
+    for i in range(bins):
+        width = min(128, share - 128 * i)
+        following, next_turned = tile, now_turned
+        if i + 1 < bins:
+            following = grads[own_rows, 128 * (i + 1) : 128 * (i + 2)].astype(f32)
+            next_turned = pltpu.roll(following, back_shift, axis=1)
+        late = jnp.where(halves < 128 - shift, now_turned, next_turned)
+        out_first[:, 128 * i : 128 * i + width] = jnp.where(y == 0, tile, late)[:, :width]
+        tile, now_turned = following, next_turned
+    first_out = local(out_first, first_ref, 0)
+    second_swap.wait()
+    for m in range(depth // 128):
+        at = slice(128 * m, 128 * (m + 1))
+        mine = seconds[pl.ds(pl.multiple_of(own_second + core * h, h), h), at].astype(f32)
+        theirs = swap[1, :, at].astype(f32)
+        set_0 = jnp.where(core == 0, mine, theirs)
+        set_1 = jnp.where(core == 0, theirs, mine)
+        out_second[:, 256 * m : 256 * m + 128] = jnp.where(
+            halves < h, set_0, pltpu.roll(set_1, h, axis=1)
+        )
+        out_second[:, 256 * m + 128 : 256 * m + 256] = jnp.where(
+            halves < h, pltpu.roll(set_0, h, axis=1), set_1
+        )
+    second_out = local(out_second, second_ref, 1)
+
+    def whole(route, buf, other_buf, parts, last):
+        if route == last:
+            return lambda n: other_buf.at[pl.ds(0, n), :]
+        first, count = parts[route]
+        return lambda n: buf.at[pl.ds(0, n), pl.ds(first * 128, count * 128)]
+
+    for route in range(last_in + 1):
+        unit = pair if route == last_in else h
+        ways_in.drain(route, whole(route, wbuf, w2buf, parts_in, last_in), unit, send_sems)
+    for route in range(last_out + 1):
+        unit = pair if route == last_out else h
+        sent = whole(route, grads, seconds, parts_out, last_out)((nz * nx * ny - 1) * unit)
+        pltpu.make_async_copy(sent, sent, sum_send_sems.at[route]).wait()
+
+    @pl.when(y == 1)
+    def _():
+        fine_halo.wait_send()
+        coarse_halo.wait_send()
+
+    first_out.wait()
+    second_out.wait()
+
+
+def per_device_by_chips(
+    grid, proposal_boxes, level_plan, fine_map, coarse_map, first_weight, second_weight, upstream
+):
+    nz, nx, ny, cores = grid
+    chips = nz * nx
+    props = level_plan.shape[1]
+    capacity = props // ny
+    fine_tile, coarse = fine_map[0], coarse_map[0]
+    fine_rows, fine_cols, channels = fine_tile.shape
+    coarse_rows = coarse.shape[0]
+    share, h = first_weight.shape
+    feats = share * ny
+    bins = max(-(-((t + 1) * share) // 128) - t * share // 128 for t in range(ny))
+    lanes = bins * 128
+    hidden_size = upstream.shape[2]
+    depth = second_weight.shape[0] // cores
+    pair = cores * h
+    low, f32 = jnp.bfloat16, jnp.float32
+    sizes = (nz, nx, ny)
+    parts_out = cut(bins, SCATTER_SHARES)
+    slot_counts = [sum(slots_of(sizes, order)) for order in SCATTER_ORDERS]
+    rows_all = chips * h
+    batch = cores * capacity
+    q = chips * ny
+    dma = pltpu.SemaphoreType.DMA
+    anywhere = pl.BlockSpec(memory_space=pl.ANY)
+    vmem = pl.BlockSpec(memory_space=pltpu.VMEM)
+    slot_shapes = [
+        (n, h, parts_out[i][1] * 128) if i < len(parts_out) else (n, pair, depth)
+        for i, n in enumerate(slot_counts)
+    ]
+    first, second = pl.pallas_call(
+        functools.partial(step_kernel, grid),
+        out_shape=(
+            jax.ShapeDtypeStruct((h, share), f32),
+            jax.ShapeDtypeStruct((h, cores * depth), f32),
+        ),
+        in_specs=[vmem, vmem] + [anywhere] * 5,
+        out_specs=(anywhere, anywhere),
+        scratch_shapes=[
+            pltpu.VMEM((h, share), low),
+            pltpu.VMEM((h, cores * depth), low),
+            pltpu.VMEM((cores, h, depth), low),
+            pltpu.VMEM((ny * rows_all, lanes), low),
+            pltpu.VMEM((ny * hidden_size, depth), low),
+            pltpu.VMEM((fine_rows + HALO, fine_cols, channels), low),
+            pltpu.VMEM((coarse_rows + HALO, coarse.shape[1], channels), low),
+            pltpu.VMEM((fine_rows + coarse_rows + 2 * HALO, fine_cols, channels), f32),
+            pltpu.VMEM((ROWS_PAD * GROUP, 128), f32),
+            pltpu.VMEM((batch, feats), low),
+            pltpu.VMEM((props, hidden_size), low),
+            pltpu.VMEM((batch, hidden_size), low),
+            pltpu.VMEM((hidden_size, batch), low),
+            pltpu.VMEM((rows_all, batch), f32),
+            pltpu.VMEM((rows_all, batch), f32),
+            pltpu.VMEM((rows_all, batch), low),
+            pltpu.VMEM((rows_all, batch), low),
+            pltpu.VMEM((ny * rows_all, lanes), low),
+            pltpu.VMEM((ny * hidden_size, depth), low),
+            pltpu.VMEM((h, share), f32),
+            pltpu.VMEM((h, cores * depth), f32),
+            pltpu.VMEM((2, h, depth), low),
+            pltpu.VMEM((8, capacity), jnp.int32),
+            pltpu.VMEM((8, capacity), f32),
+            pltpu.SMEM((8, capacity), jnp.int32),
+            pltpu.SMEM((8, capacity), f32),
+            dma((7,)),
+            dma((len(GATHER_ORDERS), 6)),
+            dma((len(GATHER_ORDERS), q)),
+            dma((len(SCATTER_ORDERS),)),
+            dma((sum(slot_counts),)),
+            dma((6,)),
+            dma((6,)),
+        ]
+        + [pltpu.VMEM(shape, low) for shape in slot_shapes],
+        compiler_params=pltpu.CompilerParams(
+            collective_id=0, has_side_effects=True, vmem_limit_bytes=64000 * 1024
+        ),
+        name="step",
+    )(
+        proposal_boxes[0],
+        level_plan,
+        first_weight.T,
+        second_weight.T,
+        upstream[0],
+        fine_tile,
+        coarse,
+    )
+    return (first.T, second.T)
+
+
 def solution(mesh):
     placed = (
         P("dp", None, None),
@@ -254,8 +1125,13 @@
         P("tile", "dp"),
         P("dp", None, None),
     )
+    grid = chip_grid(mesh)
+    tiles = mesh.shape["tile"]
+    body = per_device_by_bands
+    if grid is not None and tiles == 2 and grid[1] <= 2 and grid[2] == 2:
+        body = functools.partial(per_device_by_chips, (grid[0], grid[1], tiles, grid[2]))
     return jax.shard_map(
-        per_device,
+        body,
         mesh=mesh,
         in_specs=placed,
         out_specs=(P("tile", "dp"), P("tile", "dp")),

time: 264 us -> 142 us (0.54)
  waiting for transfers between devices: 174 us -> 0 us
  Pallas kernels: 13.2 us -> 137 us
  matrix products: 24 us -> 0 us
  other arithmetic: 21.3 us -> 0 us
  between operations: 14.4 us -> 0.64 us
  local copies, waits for them, and re-layouts: 14.1 us -> 3.66 us
    pallas_call x1, Pallas kernels: 13.2 us -> 137 us  [per_device_by_chips(): pl.pallas_call(functools.partial(step_kernel, grid), out_shape=(jax.Shape...]
    reduce_scatter x1 -> x0, waiting for transfers between devices: 93.3 us -> none  [per_device(): lax.psum_scatter(jnp.concatenate([first_part, second_part], axis=1), 'dp'...]
    ppermute x4 -> x0, waiting for transfers between devices: 80.9 us -> none  [the longest x3 56.4 us: from_ahead(): lax.ppermute(block, axis, [(i, (i - distance) % size) for i in range(size)])]
    dot_general x5 -> x0, matrix products: 24 us -> none  [the longest x1 9.24 us: per_device(): lax.dot_general(pre_grad, own_feats, over_rows, preferred_element_type=jn...]
    concatenate x4 -> x0, other arithmetic: 18.2 us -> none  [the longest x1 8.77 us: per_device(): jnp.concatenate([fine_tile, below_rows[:, :fine_cols], jnp.pad(coarse, si...]
    dynamic_update_slice x1 -> x0, local copies, waits for them, and re-layouts: 4.99 us -> none  [per_device(): lax.dynamic_update_slice(jnp.zeros((first_weight.shape[1], lanes), jnp.bf...]
    slice x9 -> x0, local copies, waits for them, and re-layouts: 3.36 us -> none  [the longest x1 1.22 us: per_device(): below_rows[:, :fine_cols]]
  transfers between devices with their start and end apart: 6 -> 0, of which waited for: 5 -> 0; matrix products, arithmetic and copies ran while one was open for 8% -> 0% of each run, Pallas kernels for 5% -> 0%
where the time goes in v2:
time: 142 us
  Pallas kernels  137 us (96%)
  local copies, waits for them, and re-layouts  3.66 us (3%)
    pallas_call x1, Pallas kernels, per_device_by_chips(): pl.pallas_call(functools.partial(step_kernel, grid), out_shape=(jax.Shape...  137 us
    unnamed x2, local copies, waits for them, and re-layouts  3.66 us

profile of v2, /device:TPU:0, one launch (start us, length us, event | category | flops | bytes accessed | tf_op | source)
XLA Modules:
  0.0 141.5 jit_solution(12540400299563767537)
XLA Ops:
  0.6 137.2 %step.1 = (f32[64,3136]{1,0:T(8,128)}, f32[64,512]{1,0:T(8,128)}) custom-call(s32[4,512]{1,0:T(4,128)} %bitcast.15, s32[1,512]{1,0:T(1,128)} %refs_1_.1, bf16[64,3136]{1,0:T(8,128)(2,1)} %bitcast.12, bf16[64,512]{1,0:T(8,128)(2,1)} %bitcast.14, bf16[512,1024]{1,0:T(8,128)(2,1)} %bitcast.9, bf16[42,168,128]{2,1,0:T(8,128)(2,1)} %bitcast.8, ...), custom_call_target="tpu_custom_call" | custom-call | tf_op jit(solution)/shard_map/step/pallas_call | solution.py:1058
  137.9 2.1 %copy.11 = f32[3136,64]{0,1:T(8,128)} copy(f32[3136,64]{0,1:T(8,128)} %bitcast.10) | data formatting | bytes 1605632
  140.0 1.6 %copy.12 = f32[512,64]{0,1:T(8,128)} copy(f32[512,64]{0,1:T(8,128)} %bitcast.13) | data formatting | bytes 262144

commit v3 on v2

--- a/solution.py
+++ b/solution.py
@@ -521,7 +521,7 @@
 SCATTER_ORDERS = ((2, 0, 1), (0, 1, 2), (1, 2, 0), (2, 0, 1))
 SCATTER_SHARES = (6, 16, 3)
 HALO_AFTER = 4
-EARLY, DURING, LAST = 18, 30, 8
+EARLY, DURING = 18, 30
 GATHER_CODES = {
     (4, 2, 2): (
         84, 0, 56, 28, 1, 85, 58, 88, 4, 8, 57, 89, 29, 9, 36, 92, 32, 5, 86, 40, 64, 93, 97,
@@ -578,8 +578,6 @@
         pres,
         grads,
         seconds,
-        out_first,
-        out_second,
         swap,
         cells_v,
         geo_v,
@@ -592,8 +590,8 @@
         sum_recv_sems,
         core_send,
         core_recv,
-    ) = refs[9:42]
-    slot_refs = refs[42:]
+    ) = refs[9:40]
+    slot_refs = refs[40:]
     nz, nx, ny, cores = grid
     sizes = (nz, nx, ny)
     dp = lax.axis_index("dp")
@@ -692,12 +690,14 @@
 
     last_in = len(GATHER_SHARES)
     last_out = len(SCATTER_SHARES)
+    cols_in = depth // (len(GATHER_ORDERS) - last_in)
+    cols_out = depth // (len(SCATTER_ORDERS) - last_out)
     loads_in = [
-        (order, parts_in[i][1] if i < last_in else depth * pair // (h * 128))
+        (order, parts_in[i][1] if i < last_in else cols_in * pair // (h * 128))
         for i, order in enumerate(GATHER_ORDERS)
     ]
     loads_out = [
-        (order, parts_out[i][1] if i < last_out else depth * pair // (h * 128))
+        (order, parts_out[i][1] if i < last_out else cols_out * pair // (h * 128))
         for i, order in enumerate(SCATTER_ORDERS)
     ]
     halo_load = HALO * (fine_cols + coarse_cols) // h
@@ -709,9 +709,10 @@
         sum_events = arrival_order(sizes, loads_out, (0, ()))[0][::-1]
 
     def gather_ref(route):
-        if route == last_in:
+        if route >= last_in:
             return lambda q: w2buf.at[
-                rows(q[2] * hidden_size + (q[0] * nx + q[1]) * pair, pair), :
+                rows(q[2] * hidden_size + (q[0] * nx + q[1]) * pair, pair),
+                pl.ds((route - last_in) * cols_in, cols_in),
             ]
         first, count = parts_in[route]
         return lambda q: wbuf.at[
@@ -732,8 +733,11 @@
     )
     own = [e for e in events if e[1] == (0, 0, 0)]
     todo = [e for e in events if e[1] != (0, 0, 0)]
+    events = own + todo
+    swapped = False
     for n, event in enumerate(own):
-        if event[0] == last_in:
+        if event[0] >= last_in and not swapped:
+            swapped = True
             w2_swap.wait()
         gather(event)
         if n + 1 == HALO_AFTER:
@@ -806,6 +810,14 @@
 
     for event in todo[:EARLY]:
         gather(event)
+    up_swap.wait()
+
+    def turn_up(i, carry):
+        at = rows(i * 128, 128)
+        uptb[at, :] = upb[:, at].astype(f32).T.astype(low)
+        return carry
+
+    lax.fori_loop(0, hidden_size // 128, turn_up, 0)
 
     @pl.when(y == 0)
     def _():
@@ -828,7 +840,6 @@
 
     groups = capacity // GROUP
     during = todo[EARLY : EARLY + DURING]
-    todo = todo[EARLY + DURING :]
     shape = (ROWS_PAD, REACH * WIN)
     k = lax.broadcasted_iota(jnp.int32, shape, 0).astype(f32)
     i_bin = jnp.floor((k + 0.5) * (1.0 / BINS))
@@ -873,41 +884,36 @@
     lax.fori_loop(0, groups, crop_group, 0)
     crop_copy((groups - 1) * GROUP, GROUP).start()
 
-    for event in todo[:-LAST]:
-        gather(event)
-    up_swap.wait()
-
-    def turn_up(i, carry):
-        at = rows(i * 128, 128)
-        uptb[at, :] = upb[:, at].astype(f32).T.astype(low)
-        return carry
-
-    lax.fori_loop(0, hidden_size // 128, turn_up, 0)
-    for event in todo[-LAST:]:
-        gather(event)
+    def hide(ahead, route, begun):
+        t = y if ahead == 0 else 1 - y
+        first, count = parts_in[route]
+        from_at = (starts[0] + t * (starts[1] - starts[0]) + first) * 128
+        part = lax.dot_general(
+            wbuf[rows(t * all_rows, all_rows), first * 128 : (first + count) * 128],
+            crops[:, pl.ds(pl.multiple_of(from_at, 128), count * 128)],
+            NT,
+            preferred_element_type=f32,
+        )
+        hidden[...] = hidden[...] + part if begun else part
+
+    ends = {(rel[2], route): i for i, (route, rel) in enumerate(events) if route < last_in}
+    ready = [(i, key) for key, i in ends.items()]
+    passed = len(own) + EARLY + DURING
+    waited, begun = False, False
+    for i in range(passed - 1, len(events)):
+        if i >= passed:
+            gather(events[i])
+        for key in [k for end, k in sorted(ready) if end == i or (i == passed - 1 and end < i)]:
+            if not waited:
+                waited = True
+                crop_copy(0, capacity).wait()
+            hide(*key, begun)
+            begun = True
     for t in range(ny):
         part = jnp.dot(
             upb[...], w2buf[t * hidden_size : (t + 1) * hidden_size, :], preferred_element_type=f32
         )
         back[t * depth : (t + 1) * depth, :] = part.T
-    crop_copy(0, capacity).wait()
-
-    chunk = 640 if lanes % 640 == 0 else 128
-    hidden[...] = jnp.zeros_like(hidden)
-    for t in range(ny):
-
-        def hide(i, carry, t=t):
-            at = pl.multiple_of(i * chunk, 128)
-            from_at = pl.multiple_of(starts[t] * 128 + i * chunk, 128)
-            hidden[...] += lax.dot_general(
-                wbuf[t * all_rows : (t + 1) * all_rows, pl.ds(at, chunk)],
-                crops[:, pl.ds(from_at, chunk)],
-                NT,
-                preferred_element_type=f32,
-            )
-            return carry
-
-        lax.fori_loop(0, lanes // chunk, hide, 0)
 
     def gelu(i, carry):
         at = rows(i * 32, 32)
@@ -919,9 +925,10 @@
     lax.fori_loop(0, hidden.shape[0] // 32, gelu, 0)
 
     def sum_ref(route):
-        if route == last_out:
+        if route >= last_out:
             return lambda q: seconds.at[
-                rows(q[2] * hidden_size + (q[0] * nx + q[1]) * pair, pair), :
+                rows(q[2] * hidden_size + (q[0] * nx + q[1]) * pair, pair),
+                pl.ds((route - last_out) * cols_out, cols_out),
             ]
         first, count = parts_out[route]
         return lambda q: grads.at[
@@ -958,10 +965,10 @@
 
     made = set()
     for route, rel in sum_events:
-        need = (route, rel[2] if route < last_out else 0)
+        need = (route, rel[2]) if route < last_out else last_out
         if need not in made:
             made.add(need)
-            if route == last_out:
+            if route >= last_out:
                 make_seconds()
             else:
                 make_grads(y if rel[2] == 0 else 1 - y, route)
@@ -969,50 +976,29 @@
             route, rel, sum_ref(route), slot_refs[route], add, sum_send_sems, sum_recv_sems
         )
 
+    first_out = local(grads.at[own_rows, :], first_ref, 0)
     own_second = y * hidden_size + chip * pair
     swap[0] = seconds[pl.ds(pl.multiple_of(own_second + other * h, h), h), :]
     second_swap = remote(swap.at[0], swap.at[1], 5, partner)
     second_swap.start()
-    tile = grads[own_rows, 0:128].astype(f32)
-    back_shift = (128 - shift) % 128
-    now_turned = pltpu.roll(tile, back_shift, axis=1)
-    for i in range(bins):
-        width = min(128, share - 128 * i)
-        following, next_turned = tile, now_turned
-        if i + 1 < bins:
-            following = grads[own_rows, 128 * (i + 1) : 128 * (i + 2)].astype(f32)
-            next_turned = pltpu.roll(following, back_shift, axis=1)
-        late = jnp.where(halves < 128 - shift, now_turned, next_turned)
-        out_first[:, 128 * i : 128 * i + width] = jnp.where(y == 0, tile, late)[:, :width]
-        tile, now_turned = following, next_turned
-    first_out = local(out_first, first_ref, 0)
-    second_swap.wait()
-    for m in range(depth // 128):
-        at = slice(128 * m, 128 * (m + 1))
-        mine = seconds[pl.ds(pl.multiple_of(own_second + core * h, h), h), at].astype(f32)
-        theirs = swap[1, :, at].astype(f32)
-        set_0 = jnp.where(core == 0, mine, theirs)
-        set_1 = jnp.where(core == 0, theirs, mine)
-        out_second[:, 256 * m : 256 * m + 128] = jnp.where(
-            halves < h, set_0, pltpu.roll(set_1, h, axis=1)
-        )
-        out_second[:, 256 * m + 128 : 256 * m + 256] = jnp.where(
-            halves < h, pltpu.roll(set_0, h, axis=1), set_1
-        )
-    second_out = local(out_second, second_ref, 1)
-
-    def whole(route, buf, other_buf, parts, last):
-        if route == last:
-            return lambda n: other_buf.at[pl.ds(0, n), :]
+    mine_out = local(
+        seconds.at[pl.ds(pl.multiple_of(own_second + core * h, h), h), :], second_ref.at[core], 1
+    )
+
+    def whole(route, buf, other_buf, parts, last, cols):
+        if route >= last:
+            return lambda n: other_buf.at[pl.ds(0, n), pl.ds((route - last) * cols, cols)]
         first, count = parts[route]
         return lambda n: buf.at[pl.ds(0, n), pl.ds(first * 128, count * 128)]
 
-    for route in range(last_in + 1):
-        unit = pair if route == last_in else h
-        ways_in.drain(route, whole(route, wbuf, w2buf, parts_in, last_in), unit, send_sems)
-    for route in range(last_out + 1):
-        unit = pair if route == last_out else h
-        sent = whole(route, grads, seconds, parts_out, last_out)((nz * nx * ny - 1) * unit)
+    for route in range(len(GATHER_ORDERS)):
+        unit = pair if route >= last_in else h
+        part = whole(route, wbuf, w2buf, parts_in, last_in, cols_in)
+        ways_in.drain(route, part, unit, send_sems)
+    for route in range(len(SCATTER_ORDERS)):
+        unit = pair if route >= last_out else h
+        part = whole(route, grads, seconds, parts_out, last_out, cols_out)
+        sent = part((nz * nx * ny - 1) * unit)
         pltpu.make_async_copy(sent, sent, sum_send_sems.at[route]).wait()
 
     @pl.when(y == 1)
@@ -1020,8 +1006,43 @@
         fine_halo.wait_send()
         coarse_halo.wait_send()
 
+    second_swap.wait()
+    theirs_out = local(swap.at[1], second_ref.at[other], 2)
     first_out.wait()
-    second_out.wait()
+    mine_out.wait()
+    theirs_out.wait()
+
+
+def finish_kernel(shift, sums_ref, sets_ref, first_ref, second_ref):
+    y = lax.axis_index("tile")
+    h, share = first_ref.shape
+    depth = sets_ref.shape[2]
+    bins = sums_ref.shape[1] // 128
+    f32 = jnp.float32
+    halves = lax.broadcasted_iota(jnp.int32, (h, 128), 1)
+    back_shift = (128 - shift) % 128
+
+    def turned(i):
+        tile = sums_ref[:, 128 * i : 128 * (i + 1)].astype(f32)
+        return tile, pltpu.roll(tile, back_shift, axis=1)
+
+    now = turned(0)
+    for i in range(bins):
+        width = min(128, share - 128 * i)
+        following = turned(i + 1) if i + 1 < bins else now
+        late = jnp.where(halves < 128 - shift, now[1], following[1])
+        first_ref[:, 128 * i : 128 * i + width] = jnp.where(y == 0, now[0], late)[:, :width]
+        now = following
+    for m in range(depth // 128):
+        at = slice(128 * m, 128 * (m + 1))
+        set_0 = sets_ref[0, :, at].astype(f32)
+        set_1 = sets_ref[1, :, at].astype(f32)
+        second_ref[:, 256 * m : 256 * m + 128] = jnp.where(
+            halves < h, set_0, pltpu.roll(set_1, h, axis=1)
+        )
+        second_ref[:, 256 * m + 128 : 256 * m + 256] = jnp.where(
+            halves < h, pltpu.roll(set_0, h, axis=1), set_1
+        )
 
 
 def per_device_by_chips(
@@ -1052,14 +1073,16 @@
     anywhere = pl.BlockSpec(memory_space=pl.ANY)
     vmem = pl.BlockSpec(memory_space=pltpu.VMEM)
     slot_shapes = [
-        (n, h, parts_out[i][1] * 128) if i < len(parts_out) else (n, pair, depth)
+        (n, h, parts_out[i][1] * 128)
+        if i < len(parts_out)
+        else (n, pair, depth // (len(SCATTER_ORDERS) - len(parts_out)))
         for i, n in enumerate(slot_counts)
     ]
-    first, second = pl.pallas_call(
+    sums, sets = pl.pallas_call(
         functools.partial(step_kernel, grid),
         out_shape=(
-            jax.ShapeDtypeStruct((h, share), f32),
-            jax.ShapeDtypeStruct((h, cores * depth), f32),
+            jax.ShapeDtypeStruct((h, lanes), low),
+            jax.ShapeDtypeStruct((cores, h, depth), low),
         ),
         in_specs=[vmem, vmem] + [anywhere] * 5,
         out_specs=(anywhere, anywhere),
@@ -1083,8 +1106,6 @@
             pltpu.VMEM((rows_all, batch), low),
             pltpu.VMEM((ny * rows_all, lanes), low),
             pltpu.VMEM((ny * hidden_size, depth), low),
-            pltpu.VMEM((h, share), f32),
-            pltpu.VMEM((h, cores * depth), f32),
             pltpu.VMEM((2, h, depth), low),
             pltpu.VMEM((8, capacity), jnp.int32),
             pltpu.VMEM((8, capacity), f32),
@@ -1112,6 +1133,17 @@
         fine_tile,
         coarse,
     )
+    shift = share - 128 * min(share // 128, feats // 128 - bins)
+    first, second = pl.pallas_call(
+        functools.partial(finish_kernel, shift),
+        out_shape=(
+            jax.ShapeDtypeStruct((h, share), f32),
+            jax.ShapeDtypeStruct((h, cores * depth), f32),
+        ),
+        in_specs=[vmem, vmem],
+        out_specs=(vmem, vmem),
+        name="finish",
+    )(sums, sets)
     return (first.T, second.T)
 
 

time: 142 us -> 136 us (0.958)
  local copies, waits for them, and re-layouts: 3.66 us -> 0 us
  Pallas kernels: 137 us -> 135 us
    pallas_call x1, Pallas kernels: 137 us -> 133 us  [per_device_by_chips(): pl.pallas_call(functools.partial(step_kernel, grid), out_shape=(jax.Shape...]
    unnamed x2 -> x0, local copies, waits for them, and re-layouts: 3.66 us -> none
    pallas_call x0 -> x1, Pallas kernels: none -> 2.13 us  [per_device_by_chips(): pl.pallas_call(functools.partial(finish_kernel, shift), out_shape=(jax.Sh...]
where the time goes in v3:
time: 136 us
  Pallas kernels  135 us (99%)
    pallas_call x1, Pallas kernels, per_device_by_chips(): pl.pallas_call(functools.partial(step_kernel, grid), out_shape=(jax.Shape...  133 us

profile of v3, /device:TPU:0, one launch (start us, length us, event | category | flops | bytes accessed | tf_op | source)
XLA Modules:
  0.0 135.9 jit_solution(9513976540575787154)
XLA Ops:
  0.6 133.2 %step.1 = (bf16[64,3200]{1,0:T(8,128)(2,1)}, bf16[2,64,256]{2,1,0:T(8,128)(2,1)}) custom-call(s32[4,512]{1,0:T(4,128)} %bitcast.13, s32[1,512]{1,0:T(1,128)} %refs_1_.1, bf16[64,3136]{1,0:T(8,128)(2,1)} %bitcast.11, bf16[64,512]{1,0:T(8,128)(2,1)} %bitcast.12, bf16[512,1024]{1,0:T(8,128)(2,1)} %bitcast.9, bf16[42,168,128]{2,1,0:T(8,128)(2,1)} %bitcast.8, ...), custom_call_target="tpu_custom_call" | custom-call | tf_op jit(solution)/shard_map/step/pallas_call | solution.py:1081
  133.8 2.1 %finish.1 = (f32[64,3136]{1,0:T(8,128)}, f32[64,512]{1,0:T(8,128)}) custom-call(bf16[64,3200]{1,0:T(8,128)(2,1)} %get-tuple-element.6.sums_ref, bf16[2,64,256]{2,1,0:T(8,128)(2,1)} %get-tuple-element.7.sets_ref), custom_call_target="tpu_custom_call" | custom-call | tf_op jit(solution)/shard_map/finish/pallas_call | solution.py:1137

commit v4 on v3

--- a/solution.py
+++ b/solution.py
@@ -516,30 +516,36 @@
     return [(a, b - a) for a, b in zip(edges, edges[1:])]
 
 
-GATHER_ORDERS = ((2, 0, 1), (0, 1, 2), (1, 2, 0), (2, 0, 1))
-GATHER_SHARES = (10, 11, 4)
-SCATTER_ORDERS = ((2, 0, 1), (0, 1, 2), (1, 2, 0), (2, 0, 1))
-SCATTER_SHARES = (6, 16, 3)
-HALO_AFTER = 4
-EARLY, DURING = 18, 30
+GATHER_ORDERS = ((2, 0, 1), (0, 1, 2), (1, 2, 0), (2, 0, 1), (0, 1, 2))
+GATHER_SHARES = (13, 9, 3)
+SCATTER_ORDERS = ((2, 0, 1), (0, 1, 2), (0, 1, 2), (1, 2, 0), (2, 0, 1))
+SCATTER_SHARES = (6, 8, 8, 3)
+HALO_AFTER = 2
+EARLY, DURING = 15, 41
+CROP_AT = (
+        0, 1, 1, 1, 1, 2, 2, 2, 2, 2, 4, 4, 4, 4, 6, 6, 6, 6, 7, 7, 7, 8, 8, 8, 9, 9, 10, 10,
+        10, 10, 10, 12, 12, 12, 12, 13, 13, 13, 14, 15, 15
+)
 GATHER_CODES = {
     (4, 2, 2): (
-        84, 0, 56, 28, 1, 85, 58, 88, 4, 8, 57, 89, 29, 9, 36, 92, 32, 5, 86, 40, 64, 93, 97,
-        16, 59, 12, 30, 38, 44, 65, 100, 37, 90, 24, 87, 17, 48, 13, 10, 61, 101, 63, 50, 34,
-        18, 7, 66, 20, 42, 73, 96, 3, 2, 62, 6, 49, 26, 31, 60, 52, 39, 45, 104, 33, 95, 46, 69,
-        25, 108, 21, 67, 91, 14, 68, 105, 109, 106, 41, 77, 54, 82, 76, 74, 71, 72, 53, 23, 94,
-        75, 11, 111, 22, 70, 102, 19, 81, 107, 110, 27, 35, 99, 47, 98, 103, 15, 80, 79, 51, 78,
-        43, 55, 83
+        0, 56, 84, 112, 28, 1, 120, 116, 32, 8, 128, 36, 58, 4, 124, 118, 136, 40, 132, 16, 12,
+        38, 122, 34, 57, 85, 62, 86, 44, 9, 48, 20, 70, 24, 5, 60, 129, 64, 138, 52, 65, 134, 2,
+        50, 13, 42, 59, 30, 68, 17, 66, 72, 125, 10, 41, 54, 37, 25, 21, 88, 14, 26, 46, 92, 80,
+        119, 121, 74, 89, 11, 93, 133, 33, 82, 105, 63, 97, 18, 22, 61, 39, 78, 87, 6, 53, 73,
+        130, 7, 29, 104, 96, 101, 109, 126, 113, 137, 71, 108, 100, 114, 69, 49, 139, 67, 19,
+        76, 117, 55, 27, 51, 23, 45, 75, 15, 43, 3, 31, 123, 94, 47, 35, 103, 111, 131, 81, 77,
+        135, 91, 107, 95, 79, 106, 127, 115, 90, 110, 99, 83, 102, 98
     ),
 }
 SCATTER_CODES = {
     (4, 2, 2): (
-        111, 26, 78, 23, 94, 51, 47, 106, 43, 35, 55, 99, 82, 37, 22, 80, 107, 110, 77, 81, 103,
-        79, 18, 74, 27, 53, 109, 98, 11, 69, 73, 76, 83, 45, 24, 108, 7, 102, 101, 87, 61, 19,
-        90, 95, 49, 75, 54, 66, 68, 25, 15, 100, 71, 63, 39, 104, 20, 70, 50, 72, 105, 10, 16,
-        14, 91, 46, 65, 42, 41, 17, 2, 67, 92, 97, 31, 64, 33, 93, 29, 88, 21, 96, 6, 3, 52, 34,
-        13, 48, 89, 9, 5, 12, 62, 40, 4, 38, 85, 60, 44, 8, 59, 1, 30, 32, 36, 58, 57, 86, 0,
-        56, 28, 84
+        6, 138, 110, 39, 106, 123, 35, 109, 108, 83, 22, 14, 107, 105, 51, 139, 27, 23, 75, 98,
+        111, 131, 102, 55, 19, 130, 7, 135, 11, 101, 26, 134, 47, 94, 43, 137, 15, 99, 71, 37,
+        73, 18, 100, 82, 53, 25, 103, 79, 127, 63, 93, 90, 41, 20, 136, 104, 97, 54, 12, 74, 21,
+        49, 81, 33, 77, 91, 17, 96, 133, 129, 132, 10, 118, 3, 46, 115, 122, 125, 50, 126, 67,
+        13, 24, 16, 119, 65, 78, 9, 42, 4, 128, 92, 59, 52, 70, 80, 89, 45, 114, 34, 121, 62,
+        31, 95, 69, 66, 8, 72, 44, 5, 61, 57, 38, 85, 2, 120, 124, 117, 88, 87, 76, 1, 48, 116,
+        113, 58, 68, 40, 64, 60, 86, 30, 32, 29, 36, 0, 84, 56, 112, 28
     ),
 }
 
@@ -675,18 +681,7 @@
         before = turned
         wbuf[own_rows, 128 * i : 128 * (i + 1)] = jnp.where(y == 0, now, late).astype(low)
 
-    w2_copy.wait()
-    for m in range(depth // 128):
-        a = w2_in[:, 256 * m : 256 * m + 128].astype(f32)
-        b = w2_in[:, 256 * m + 128 : 256 * m + 256].astype(f32)
-        at = slice(128 * m, 128 * (m + 1))
-        w2_sets[0, :, at] = jnp.where(halves < h, a, pltpu.roll(b, h, axis=1)).astype(low)
-        w2_sets[1, :, at] = jnp.where(halves < h, pltpu.roll(a, h, axis=1), b).astype(low)
-    w2_rows = pl.ds(pl.multiple_of(y * hidden_size + chip * pair + core * h, h), h)
-    w2buf[w2_rows, :] = w2_sets[core]
-
     pl.semaphore_wait(barrier, peers)
-    w2_swap = remote(w2_sets.at[other], w2buf.at[w2_rows, :], 0, partner)
 
     last_in = len(GATHER_SHARES)
     last_out = len(SCATTER_SHARES)
@@ -723,7 +718,6 @@
         route, rel = event
         ways_in.gather(route, rel, gather_ref(route), send_sems, recv_sems)
 
-    w2_swap.start()
     below = ways_in.device(2, 1)
     fine_halo = remote(
         fine_ref.at[pl.ds(0, HALO)], fine_low.at[pl.ds(fine_rows, HALO)], 1, below
@@ -733,19 +727,33 @@
     )
     own = [e for e in events if e[1] == (0, 0, 0)]
     todo = [e for e in events if e[1] != (0, 0, 0)]
-    events = own + todo
-    swapped = False
-    for n, event in enumerate(own):
-        if event[0] >= last_in and not swapped:
-            swapped = True
-            w2_swap.wait()
+    own.sort(key=lambda e: e[0] >= last_in)
+    for n, event in enumerate(own[:last_in]):
         gather(event)
-        if n + 1 == HALO_AFTER:
+        if n + 1 == min(HALO_AFTER, last_in):
 
             @pl.when(y == 1)
             def _():
                 fine_halo.start()
                 coarse_halo.start()
+
+    w2_copy.wait()
+    for m in range(depth // 128):
+        a = w2_in[:, 256 * m : 256 * m + 128].astype(f32)
+        b = w2_in[:, 256 * m + 128 : 256 * m + 256].astype(f32)
+        at = slice(128 * m, 128 * (m + 1))
+        w2_sets[0, :, at] = jnp.where(halves < h, a, pltpu.roll(b, h, axis=1)).astype(low)
+        w2_sets[1, :, at] = jnp.where(halves < h, pltpu.roll(a, h, axis=1), b).astype(low)
+    w2_rows = pl.ds(pl.multiple_of(y * hidden_size + chip * pair + core * h, h), h)
+    w2buf[w2_rows, :] = w2_sets[core]
+
+    w2_swap = remote(w2_sets.at[other], w2buf.at[w2_rows, :], 0, partner)
+    w2_swap.start()
+    w2_swap.wait()
+    for event in own[last_in:]:
+        gather(event)
+
+    events = own + todo
 
     member = jnp.logical_and(
         fields_ref[0:1, :] >= y * (4 * fine_rows), fields_ref[0:1, :] < (y + 1) * (4 * fine_rows)
@@ -856,7 +864,8 @@
 
     def crop_group(g, carry):
         for n, event in enumerate(during):
-            pl.when(g == n * groups // len(during))(functools.partial(gather, event))
+            at = CROP_AT[n] if sizes in GATHER_CODES else n * groups // len(during)
+            pl.when(g == min(at, groups - 1))(functools.partial(gather, event))
         for p in range(GROUP):
             n = g * GROUP + p
             row = jnp.clip(cells_ref[0, n], 0, wide.shape[0] - REACH)
@@ -963,7 +972,8 @@
                 uptb[...], acts[t * depth : (t + 1) * depth, :], NT, preferred_element_type=f32
             ).astype(low)
 
-    made = set()
+    own_second = y * hidden_size + chip * pair
+    made, ended, outs, swapped = set(), set(), [], False
     for route, rel in sum_events:
         need = (route, rel[2]) if route < last_out else last_out
         if need not in made:
@@ -975,15 +985,20 @@
         ways_out.scatter(
             route, rel, sum_ref(route), slot_refs[route], add, sum_send_sems, sum_recv_sems
         )
-
-    first_out = local(grads.at[own_rows, :], first_ref, 0)
-    own_second = y * hidden_size + chip * pair
-    swap[0] = seconds[pl.ds(pl.multiple_of(own_second + other * h, h), h), :]
-    second_swap = remote(swap.at[0], swap.at[1], 5, partner)
-    second_swap.start()
-    mine_out = local(
-        seconds.at[pl.ds(pl.multiple_of(own_second + core * h, h), h), :], second_ref.at[core], 1
-    )
+        if rel != (0, 0, 0):
+            continue
+        ended.add(route)
+        if route < last_out:
+            first, count = parts_out[route]
+            at = pl.ds(first * 128, count * 128)
+            outs.append(local(grads.at[own_rows, at], first_ref.at[:, at], len(outs)))
+        if not swapped and all(r in ended for r in range(last_out, len(SCATTER_ORDERS))):
+            swapped = True
+            swap[0] = seconds[pl.ds(pl.multiple_of(own_second + other * h, h), h), :]
+            second_swap = remote(swap.at[0], swap.at[1], 5, partner)
+            second_swap.start()
+            mine = seconds.at[pl.ds(pl.multiple_of(own_second + core * h, h), h), :]
+            outs.append(local(mine, second_ref.at[core], len(outs)))
 
     def whole(route, buf, other_buf, parts, last, cols):
         if route >= last:
@@ -1007,10 +1022,9 @@
         coarse_halo.wait_send()
 
     second_swap.wait()
-    theirs_out = local(swap.at[1], second_ref.at[other], 2)
-    first_out.wait()
-    mine_out.wait()
-    theirs_out.wait()
+    outs.append(local(swap.at[1], second_ref.at[other], len(outs)))
+    for copy in outs:
+        copy.wait()
 
 
 def finish_kernel(shift, sums_ref, sets_ref, first_ref, second_ref):
@@ -1111,7 +1125,7 @@
             pltpu.VMEM((8, capacity), f32),
             pltpu.SMEM((8, capacity), jnp.int32),
             pltpu.SMEM((8, capacity), f32),
-            dma((7,)),
+            dma((max(7, len(SCATTER_ORDERS) + 2),)),
             dma((len(GATHER_ORDERS), 6)),
             dma((len(GATHER_ORDERS), q)),
             dma((len(SCATTER_ORDERS),)),

time: 136 us -> 129 us (0.949)
  Pallas kernels: 135 us -> 129 us
    pallas_call x1, Pallas kernels: 133 us -> 126 us  [per_device_by_chips(): pl.pallas_call(functools.partial(step_kernel, grid), out_shape=(jax.Shape...]
where the time goes in v4:
time: 129 us
  Pallas kernels  129 us (100%)
    pallas_call x1, Pallas kernels, per_device_by_chips(): pl.pallas_call(functools.partial(step_kernel, grid), out_shape=(jax.Shape...  126 us

profile of v4, /device:TPU:0, one launch (start us, length us, event | category | flops | bytes accessed | tf_op | source)
XLA Modules:
  0.0 129.2 jit_solution(10253306852579128005)
XLA Ops:
  0.6 126.4 %step.1 = (bf16[64,3200]{1,0:T(8,128)(2,1)}, bf16[2,64,256]{2,1,0:T(8,128)(2,1)}) custom-call(s32[4,512]{1,0:T(4,128)} %bitcast.13, s32[1,512]{1,0:T(1,128)} %refs_1_.1, bf16[64,3136]{1,0:T(8,128)(2,1)} %bitcast.11, bf16[64,512]{1,0:T(8,128)(2,1)} %bitcast.12, bf16[512,1024]{1,0:T(8,128)(2,1)} %bitcast.9, bf16[42,168,128]{2,1,0:T(8,128)(2,1)} %bitcast.8, ...), custom_call_target="tpu_custom_call" | custom-call | tf_op jit(solution)/shard_map/step/pallas_call | solution.py:1095
  127.1 2.1 %finish.1 = (f32[64,3136]{1,0:T(8,128)}, f32[64,512]{1,0:T(8,128)}) custom-call(bf16[64,3200]{1,0:T(8,128)(2,1)} %get-tuple-element.6.sums_ref, bf16[2,64,256]{2,1,0:T(8,128)(2,1)} %get-tuple-element.7.sets_ref), custom_call_target="tpu_custom_call" | custom-call | tf_op jit(solution)/shard_map/finish/pallas_call | solution.py:1151

commit v5 on v4

--- a/solution.py
+++ b/solution.py
@@ -366,7 +366,7 @@
     counts, before = [], 1
     for j in range(3):
         n = sizes[order[j]]
-        counts.append(before * (2 * n if n > 2 else 1))
+        counts.append(before * (n + 1 if n > 2 else 1))
         before *= n
     return counts
 
@@ -414,7 +414,7 @@
         return (place[0] * self.sizes[1] + place[1]) * self.sizes[2] + place[2]
 
     def direction(self, axis, step):
-        return 2 * axis + (1 if step > 0 else 0)
+        return axis + 1 if axis else (1 if step > 0 else 0)
 
     def drain(self, route, whole, unit, sems):
         order, before = self.orders[route], 1
@@ -461,14 +461,14 @@
 
         when(self.valid(rel), body)
 
-    def slot(self, route, phase, side, place):
+    def slot(self, route, phase, side, place, here):
         order, counts = self.orders[route], self.slot_counts[route]
         index = 0
         for j in range(phase):
             index = index * self.sizes[order[j]] + place[order[j]]
         n = self.sizes[order[phase]]
         if n > 2:
-            index = (index * n + place[order[phase]]) * 2 + (1 if side > 0 else 0)
+            index = index * (n + 1) + (n if here and side > 0 else place[order[phase]])
         return sum(counts[:phase]) + index
 
     def scatter(self, route, rel, ref_of, slots, add, send_sems, recv_sems):
@@ -479,7 +479,7 @@
             ref = ref_of(place)
             base = self.slot_base[route]
             for phase, axis, step in onward(self.sizes, order, rel):
-                slot = self.slot(route, phase, step, place)
+                slot = self.slot(route, phase, step, place, rel[axis] == 0)
 
                 def take(axis=axis, step=step, slot=slot):
                     pltpu.make_async_remote_copy(
@@ -496,7 +496,8 @@
             phase = last_axis(order, rel)
             if phase >= 0:
                 axis, step = self.back_step(order, rel)
-                slot = self.slot(route, phase, 1 if self.sizes[axis] == 2 else -step, place)
+                here = rel[axis] - step == 0
+                slot = self.slot(route, phase, -step, place, here)
                 pltpu.make_async_remote_copy(
                     src_ref=ref,
                     dst_ref=slots.at[slot],
@@ -517,35 +518,38 @@
 
 
 GATHER_ORDERS = ((2, 0, 1), (0, 1, 2), (1, 2, 0), (2, 0, 1), (0, 1, 2))
-GATHER_SHARES = (13, 9, 3)
-SCATTER_ORDERS = ((2, 0, 1), (0, 1, 2), (0, 1, 2), (1, 2, 0), (2, 0, 1))
-SCATTER_SHARES = (6, 8, 8, 3)
-HALO_AFTER = 2
-EARLY, DURING = 15, 41
+GATHER_SHARES = (12, 9, 4)
+SCATTER_ORDERS = ((2, 0, 1), (2, 0, 1), (0, 1, 2), (0, 1, 2), (1, 2, 0), (2, 0, 1))
+SCATTER_SHARES = (3, 3, 8, 8, 3)
+HALO_AFTER = 3
+EARLY, DURING = 13, 56
 CROP_AT = (
-        0, 1, 1, 1, 1, 2, 2, 2, 2, 2, 4, 4, 4, 4, 6, 6, 6, 6, 7, 7, 7, 8, 8, 8, 9, 9, 10, 10,
-        10, 10, 10, 12, 12, 12, 12, 13, 13, 13, 14, 15, 15
+        2, 2, 2, 2, 3, 3, 3, 3, 3, 4, 5, 6, 6, 7, 7, 7, 7, 7, 7, 8, 8, 8, 8, 9, 9, 9, 10, 11,
+        11, 11, 11, 11, 12, 12, 13, 13, 13, 13, 13, 13, 13, 13, 13, 13, 13, 13, 14, 15, 15, 15,
+        15, 15, 15, 15, 15, 15
 )
 GATHER_CODES = {
     (4, 2, 2): (
-        0, 56, 84, 112, 28, 1, 120, 116, 32, 8, 128, 36, 58, 4, 124, 118, 136, 40, 132, 16, 12,
-        38, 122, 34, 57, 85, 62, 86, 44, 9, 48, 20, 70, 24, 5, 60, 129, 64, 138, 52, 65, 134, 2,
-        50, 13, 42, 59, 30, 68, 17, 66, 72, 125, 10, 41, 54, 37, 25, 21, 88, 14, 26, 46, 92, 80,
-        119, 121, 74, 89, 11, 93, 133, 33, 82, 105, 63, 97, 18, 22, 61, 39, 78, 87, 6, 53, 73,
-        130, 7, 29, 104, 96, 101, 109, 126, 113, 137, 71, 108, 100, 114, 69, 49, 139, 67, 19,
-        76, 117, 55, 27, 51, 23, 45, 75, 15, 43, 3, 31, 123, 94, 47, 35, 103, 111, 131, 81, 77,
-        135, 91, 107, 95, 79, 106, 127, 115, 90, 110, 99, 83, 102, 98
+        0, 84, 112, 28, 56, 116, 4, 8, 36, 16, 120, 44, 1, 124, 32, 12, 58, 40, 24, 85, 52, 9,
+        5, 48, 20, 64, 57, 54, 46, 18, 136, 118, 62, 128, 13, 66, 17, 113, 3, 125, 38, 93, 26,
+        121, 45, 42, 60, 55, 132, 30, 22, 87, 21, 88, 2, 96, 25, 50, 34, 59, 29, 92, 49, 138,
+        89, 126, 70, 6, 14, 33, 134, 137, 97, 74, 61, 68, 11, 47, 108, 37, 105, 23, 78, 100, 7,
+        65, 63, 101, 72, 130, 104, 117, 67, 86, 10, 19, 53, 82, 122, 27, 69, 80, 109, 114, 73,
+        51, 15, 107, 95, 110, 76, 90, 75, 31, 98, 106, 41, 71, 39, 35, 43, 91, 127, 135, 94,
+        129, 77, 133, 81, 131, 139, 102, 123, 119, 111, 103, 99, 83, 79, 115
     ),
 }
 SCATTER_CODES = {
     (4, 2, 2): (
-        6, 138, 110, 39, 106, 123, 35, 109, 108, 83, 22, 14, 107, 105, 51, 139, 27, 23, 75, 98,
-        111, 131, 102, 55, 19, 130, 7, 135, 11, 101, 26, 134, 47, 94, 43, 137, 15, 99, 71, 37,
-        73, 18, 100, 82, 53, 25, 103, 79, 127, 63, 93, 90, 41, 20, 136, 104, 97, 54, 12, 74, 21,
-        49, 81, 33, 77, 91, 17, 96, 133, 129, 132, 10, 118, 3, 46, 115, 122, 125, 50, 126, 67,
-        13, 24, 16, 119, 65, 78, 9, 42, 4, 128, 92, 59, 52, 70, 80, 89, 45, 114, 34, 121, 62,
-        31, 95, 69, 66, 8, 72, 44, 5, 61, 57, 38, 85, 2, 120, 124, 117, 88, 87, 76, 1, 48, 116,
-        113, 58, 68, 40, 64, 60, 86, 30, 32, 29, 36, 0, 84, 56, 112, 28
+        43, 47, 137, 132, 55, 67, 81, 51, 71, 133, 134, 50, 35, 34, 138, 26, 89, 162, 49, 83,
+        139, 23, 18, 107, 39, 105, 22, 147, 27, 163, 63, 131, 79, 42, 95, 126, 111, 15, 129,
+        167, 103, 159, 53, 7, 14, 48, 69, 125, 19, 41, 155, 6, 46, 54, 33, 21, 20, 124, 130,
+        161, 45, 160, 99, 135, 91, 166, 158, 136, 146, 117, 77, 106, 123, 121, 25, 13, 75, 128,
+        38, 154, 12, 82, 62, 122, 151, 37, 165, 143, 61, 97, 116, 30, 109, 17, 164, 110, 40,
+        118, 127, 5, 101, 150, 157, 152, 66, 78, 98, 102, 153, 11, 70, 87, 65, 52, 44, 24, 119,
+        80, 156, 93, 4, 104, 90, 74, 144, 115, 73, 148, 94, 3, 10, 76, 108, 142, 145, 59, 31,
+        96, 16, 149, 100, 85, 36, 2, 141, 68, 32, 9, 120, 88, 86, 72, 113, 8, 114, 92, 29, 60,
+        1, 64, 57, 58, 140, 0, 112, 28, 84, 56
     ),
 }
 
@@ -670,18 +674,24 @@
 
     w_copy.wait()
     own_rows = pl.ds(pl.multiple_of(y * all_rows + chip * h, h), h)
-    before = jnp.zeros((h, 128), f32)
-    for i in range(bins):
-        width = min(128, share - 128 * i)
+
+    def turned(i):
+        width = min(128, share - 128 * i) if i >= 0 else 0
+        if width <= 0:
+            return jnp.zeros((h, 128), f32), jnp.zeros((h, 128), f32)
         now = w_in[:, 128 * i : 128 * i + width].astype(f32)
         if width < 128:
             now = jnp.concatenate([now, jnp.zeros((h, 128 - width), f32)], axis=1)
-        turned = pltpu.roll(now, shift, axis=1) if shift else now
-        late = jnp.where(halves < shift, before, turned)
-        before = turned
-        wbuf[own_rows, 128 * i : 128 * (i + 1)] = jnp.where(y == 0, now, late).astype(low)
-
-    pl.semaphore_wait(barrier, peers)
+        return now, (pltpu.roll(now, shift, axis=1) if shift else now)
+
+    def turn(first, count):
+        before = turned(first - 1)[1]
+        for i in range(first, first + count):
+            now, after = turned(i)
+            late = jnp.where(halves < shift, before, after)
+            before = after
+            wbuf[own_rows, 128 * i : 128 * (i + 1)] = jnp.where(y == 0, now, late).astype(low)
+
 
     last_in = len(GATHER_SHARES)
     last_out = len(SCATTER_SHARES)
@@ -729,6 +739,9 @@
     todo = [e for e in events if e[1] != (0, 0, 0)]
     own.sort(key=lambda e: e[0] >= last_in)
     for n, event in enumerate(own[:last_in]):
+        turn(*parts_in[event[0]])
+        if n == 0:
+            pl.semaphore_wait(barrier, peers)
         gather(event)
         if n + 1 == min(HALO_AFTER, last_in):
 
@@ -905,7 +918,16 @@
         )
         hidden[...] = hidden[...] + part if begun else part
 
-    ends = {(rel[2], route): i for i, (route, rel) in enumerate(events) if route < last_in}
+    def make_back(ahead):
+        t = y if ahead == 0 else 1 - y
+        part = jnp.dot(
+            upb[...], w2buf[rows(t * hidden_size, hidden_size), :], preferred_element_type=f32
+        )
+        back[rows(t * depth, depth), :] = part.T
+
+    ends = {
+        (rel[2], route if route < last_in else -1): i for i, (route, rel) in enumerate(events)
+    }
     ready = [(i, key) for key, i in ends.items()]
     passed = len(own) + EARLY + DURING
     waited, begun = False, False
@@ -913,17 +935,14 @@
         if i >= passed:
             gather(events[i])
         for key in [k for end, k in sorted(ready) if end == i or (i == passed - 1 and end < i)]:
+            if key[1] < 0:
+                make_back(key[0])
+                continue
             if not waited:
                 waited = True
                 crop_copy(0, capacity).wait()
             hide(*key, begun)
             begun = True
-    for t in range(ny):
-        part = jnp.dot(
-            upb[...], w2buf[t * hidden_size : (t + 1) * hidden_size, :], preferred_element_type=f32
-        )
-        back[t * depth : (t + 1) * depth, :] = part.T
-
     def gelu(i, carry):
         at = rows(i * 32, 32)
         value, slope = gelu_parts(hidden[at, :])
@@ -1126,7 +1145,7 @@
             pltpu.SMEM((8, capacity), jnp.int32),
             pltpu.SMEM((8, capacity), f32),
             dma((max(7, len(SCATTER_ORDERS) + 2),)),
-            dma((len(GATHER_ORDERS), 6)),
+            dma((len(GATHER_ORDERS), 4)),
             dma((len(GATHER_ORDERS), q)),
             dma((len(SCATTER_ORDERS),)),
             dma((sum(slot_counts),)),

time: 129 us -> 129 us (level)
  no operation moved by 1% of the time
where the time goes in v5:
time: 129 us; the launch traced here: 128 us
  Pallas kernels  128 us (99%)
    pallas_call x1, Pallas kernels, per_device_by_chips(): pl.pallas_call(functools.partial(step_kernel, grid), out_shape=(jax.Shape...  126 us

profile of v5, /device:TPU:0, one launch (start us, length us, event | category | flops | bytes accessed | tf_op | source)
XLA Modules:
  0.0 128.5 jit_solution(15907799454475981882)
XLA Ops:
  0.6 125.7 %step.1 = (bf16[64,3200]{1,0:T(8,128)(2,1)}, bf16[2,64,256]{2,1,0:T(8,128)(2,1)}) custom-call(s32[4,512]{1,0:T(4,128)} %bitcast.13, s32[1,512]{1,0:T(1,128)} %refs_1_.1, bf16[64,3136]{1,0:T(8,128)(2,1)} %bitcast.11, bf16[64,512]{1,0:T(8,128)(2,1)} %bitcast.12, bf16[512,1024]{1,0:T(8,128)(2,1)} %bitcast.9, bf16[42,168,128]{2,1,0:T(8,128)(2,1)} %bitcast.8, ...), custom_call_target="tpu_custom_call" | custom-call | tf_op jit(solution)/shard_map/step/pallas_call | solution.py:1114
  126.3 2.1 %finish.1 = (f32[64,3136]{1,0:T(8,128)}, f32[64,512]{1,0:T(8,128)}) custom-call(bf16[64,3200]{1,0:T(8,128)(2,1)} %get-tuple-element.6.sums_ref, bf16[2,64,256]{2,1,0:T(8,128)(2,1)} %get-tuple-element.7.sets_ref), custom_call_target="tpu_custom_call" | custom-call | tf_op jit(solution)/shard_map/finish/pallas_call | solution.py:1170

commit v6 on v5

--- a/solution.py
+++ b/solution.py
@@ -519,8 +519,8 @@
 
 GATHER_ORDERS = ((2, 0, 1), (0, 1, 2), (1, 2, 0), (2, 0, 1), (0, 1, 2))
 GATHER_SHARES = (12, 9, 4)
-SCATTER_ORDERS = ((2, 0, 1), (2, 0, 1), (0, 1, 2), (0, 1, 2), (1, 2, 0), (2, 0, 1))
-SCATTER_SHARES = (3, 3, 8, 8, 3)
+SCATTER_ORDERS = ((2, 0, 1), (0, 1, 2), (0, 1, 2), (1, 2, 0), (2, 0, 1))
+SCATTER_SHARES = (6, 8, 8, 3)
 HALO_AFTER = 3
 EARLY, DURING = 13, 56
 CROP_AT = (
@@ -541,15 +541,13 @@
 }
 SCATTER_CODES = {
     (4, 2, 2): (
-        43, 47, 137, 132, 55, 67, 81, 51, 71, 133, 134, 50, 35, 34, 138, 26, 89, 162, 49, 83,
-        139, 23, 18, 107, 39, 105, 22, 147, 27, 163, 63, 131, 79, 42, 95, 126, 111, 15, 129,
-        167, 103, 159, 53, 7, 14, 48, 69, 125, 19, 41, 155, 6, 46, 54, 33, 21, 20, 124, 130,
-        161, 45, 160, 99, 135, 91, 166, 158, 136, 146, 117, 77, 106, 123, 121, 25, 13, 75, 128,
-        38, 154, 12, 82, 62, 122, 151, 37, 165, 143, 61, 97, 116, 30, 109, 17, 164, 110, 40,
-        118, 127, 5, 101, 150, 157, 152, 66, 78, 98, 102, 153, 11, 70, 87, 65, 52, 44, 24, 119,
-        80, 156, 93, 4, 104, 90, 74, 144, 115, 73, 148, 94, 3, 10, 76, 108, 142, 145, 59, 31,
-        96, 16, 149, 100, 85, 36, 2, 141, 68, 32, 9, 120, 88, 86, 72, 113, 8, 114, 92, 29, 60,
-        1, 64, 57, 58, 140, 0, 112, 28, 84, 56
+        6, 138, 110, 39, 106, 123, 35, 109, 108, 83, 22, 14, 107, 105, 51, 139, 27, 23, 75, 98,
+        111, 131, 102, 55, 19, 130, 7, 135, 11, 101, 26, 134, 47, 94, 43, 137, 15, 99, 71, 37,
+        73, 18, 100, 82, 53, 25, 103, 79, 127, 63, 93, 90, 41, 20, 136, 104, 97, 54, 12, 74, 21,
+        49, 81, 33, 77, 91, 17, 96, 133, 129, 132, 10, 118, 3, 46, 115, 122, 125, 50, 126, 67,
+        13, 24, 16, 119, 65, 78, 9, 42, 4, 128, 92, 59, 52, 70, 80, 89, 45, 114, 34, 121, 62,
+        31, 95, 69, 66, 8, 72, 44, 5, 61, 57, 38, 85, 2, 120, 124, 117, 88, 87, 76, 1, 48, 116,
+        113, 58, 68, 40, 64, 60, 86, 30, 32, 29, 36, 0, 84, 56, 112, 28
     ),
 }
 
@@ -1046,36 +1044,59 @@
         copy.wait()
 
 
-def finish_kernel(shift, sums_ref, sets_ref, first_ref, second_ref):
+def finish_kernel(
+    shift, sums_ref, sets_ref, first_ref, second_ref, sums, sets, first, second, come, gone
+):
     y = lax.axis_index("tile")
     h, share = first_ref.shape
     depth = sets_ref.shape[2]
     bins = sums_ref.shape[1] // 128
     f32 = jnp.float32
-    halves = lax.broadcasted_iota(jnp.int32, (h, 128), 1)
+    chunks = come.shape[0] - 1
+    size = h // chunks
+    halves = lax.broadcasted_iota(jnp.int32, (size, 128), 1)
+    whole = lax.broadcasted_iota(jnp.int32, (h, 128), 1)
     back_shift = (128 - shift) % 128
-
-    def turned(i):
-        tile = sums_ref[:, 128 * i : 128 * (i + 1)].astype(f32)
-        return tile, pltpu.roll(tile, back_shift, axis=1)
-
-    now = turned(0)
-    for i in range(bins):
-        width = min(128, share - 128 * i)
-        following = turned(i + 1) if i + 1 < bins else now
-        late = jnp.where(halves < 128 - shift, now[1], following[1])
-        first_ref[:, 128 * i : 128 * i + width] = jnp.where(y == 0, now[0], late)[:, :width]
-        now = following
+    parts = [slice(c * size, (c + 1) * size) for c in range(chunks)]
+    loads = [
+        pltpu.make_async_copy(sums_ref.at[part, :], sums.at[part, :], come.at[c])
+        for c, part in enumerate(parts)
+    ]
+    loads.append(pltpu.make_async_copy(sets_ref, sets, come.at[chunks]))
+    for copy in loads:
+        copy.start()
+    stores = []
+    for c, part in enumerate(parts):
+        loads[c].wait()
+
+        def turned(i, part=part):
+            tile = sums[part, 128 * i : 128 * (i + 1)].astype(f32)
+            return tile, pltpu.roll(tile, back_shift, axis=1)
+
+        now = turned(0)
+        for i in range(bins):
+            width = min(128, share - 128 * i)
+            following = turned(i + 1) if i + 1 < bins else now
+            late = jnp.where(halves < 128 - shift, now[1], following[1])
+            first[part, 128 * i : 128 * i + width] = jnp.where(y == 0, now[0], late)[:, :width]
+            now = following
+        stores.append(pltpu.make_async_copy(first.at[part, :], first_ref.at[part, :], gone.at[c]))
+        stores[-1].start()
+    loads[chunks].wait()
     for m in range(depth // 128):
         at = slice(128 * m, 128 * (m + 1))
-        set_0 = sets_ref[0, :, at].astype(f32)
-        set_1 = sets_ref[1, :, at].astype(f32)
-        second_ref[:, 256 * m : 256 * m + 128] = jnp.where(
-            halves < h, set_0, pltpu.roll(set_1, h, axis=1)
+        set_0 = sets[0, :, at].astype(f32)
+        set_1 = sets[1, :, at].astype(f32)
+        second[:, 256 * m : 256 * m + 128] = jnp.where(
+            whole < h, set_0, pltpu.roll(set_1, h, axis=1)
         )
-        second_ref[:, 256 * m + 128 : 256 * m + 256] = jnp.where(
-            halves < h, pltpu.roll(set_0, h, axis=1), set_1
+        second[:, 256 * m + 128 : 256 * m + 256] = jnp.where(
+            whole < h, pltpu.roll(set_0, h, axis=1), set_1
         )
+    stores.append(pltpu.make_async_copy(second, second_ref, gone.at[chunks]))
+    stores[-1].start()
+    for copy in stores:
+        copy.wait()
 
 
 def per_device_by_chips(
@@ -1173,8 +1194,16 @@
             jax.ShapeDtypeStruct((h, share), f32),
             jax.ShapeDtypeStruct((h, cores * depth), f32),
         ),
-        in_specs=[vmem, vmem],
-        out_specs=(vmem, vmem),
+        in_specs=[anywhere, anywhere],
+        out_specs=(anywhere, anywhere),
+        scratch_shapes=[
+            pltpu.VMEM((h, lanes), low),
+            pltpu.VMEM((cores, h, depth), low),
+            pltpu.VMEM((h, share), f32),
+            pltpu.VMEM((h, cores * depth), f32),
+            dma((h // 16 + 1,)),
+            dma((h // 16 + 1,)),
+        ],
         name="finish",
     )(sums, sets)
     return (first.T, second.T)

time: 129 us -> 128 us (level)
  no operation moved by 1% of the time
where the time goes in v6:
time: 128 us
  Pallas kernels  127 us (99%)
    pallas_call x1, Pallas kernels, per_device_by_chips(): pl.pallas_call(functools.partial(step_kernel, grid), out_shape=(jax.Shape...  125 us

profile of v6, /device:TPU:0, one launch (start us, length us, event | category | flops | bytes accessed | tf_op | source)
XLA Modules:
  0.0 128.1 jit_solution(595265606380450431)
XLA Ops:
  0.6 125.3 %step.1 = (bf16[64,3200]{1,0:T(8,128)(2,1)}, bf16[2,64,256]{2,1,0:T(8,128)(2,1)}) custom-call(s32[4,512]{1,0:T(4,128)} %bitcast.13, s32[1,512]{1,0:T(1,128)} %refs_1_.1, bf16[64,3136]{1,0:T(8,128)(2,1)} %bitcast.11, bf16[64,512]{1,0:T(8,128)(2,1)} %bitcast.12, bf16[512,1024]{1,0:T(8,128)(2,1)} %bitcast.9, bf16[42,168,128]{2,1,0:T(8,128)(2,1)} %bitcast.8, ...), custom_call_target="tpu_custom_call" | custom-call | tf_op jit(solution)/shard_map/step/pallas_call | solution.py:1135
  126.0 2.1 %finish.1 = (f32[64,3136]{1,0:T(8,128)}, f32[64,512]{1,0:T(8,128)}) custom-call(bf16[64,3200]{1,0:T(8,128)(2,1)} %get-tuple-element.6.sums_ref, bf16[2,64,256]{2,1,0:T(8,128)(2,1)} %get-tuple-element.7.sets_ref), custom_call_target="tpu_custom_call" | custom-call | tf_op jit(solution)/shard_map/finish/pallas_call | solution.py:1191
